TPU v7x, 32 devices: a whole 2x2x4 slice. The times are simulated.
32 devices in a mesh: row: 8 (over z, x), col: 4 (over y, core).
Axes of the slice: x: 2, y: 2, z: 4, core: 2. Of those that a mesh axis runs over, the one named last changes fastest.
Arguments:
- pole_values: float32 [65536], P('row'), may hold values from -32768 to 32768, as said below
- weights: float32 [65536], P('row'), may hold values from 0.15 to 0.5
- centers: float32 [65536], P('col'), as said below
- offsets: float32 [65536], P('col'), may hold values from -0.1 to 0.1
- chosen: int32 [2048], replicated, may hold values from 0 to 65535
- column_pole: int32 [2, 32768], P(None, 'row'), may hold values from 0 to 65535, as said below
- eigen_blocks: bfloat16 [3072, 2, 32768], P('col', None, 'row'), may hold values from -6 to 6
Outputs:
- roots_offset: float32 [65536], P('col')
- panel: float32 [3072, 2, 2048], P(('col', 'row'))
Inputs may be any that keep to these rules, and one draw needn't show every extreme that they name: `pole_values`: ascending; consecutive poles differ by 1/4 to 7/4; every pole is a multiple of 1/128. centers[i] is the midpoint of pole_values[i] and pole_values[i + 1]; the last one is the last pole plus 1/2. `chosen`: indices of roots. `column_pole`: each of 0 to 65535 stands once.
All inputs are finite; a program needn't handle non-finite values.
Results may differ from a plain program's by a relative error of at most 0.0021.
Values may be sent and summed in bfloat16 or wider, within the bound.
A program may use at most 128 MiB of HBM per device.

v0:
```python
import jax
import jax.numpy as jnp
from jax import lax
from jax.experimental import pallas as pl
from jax.experimental.pallas import tpu as pltpu
from jax.sharding import PartitionSpec as P

ITERS = 3
LANES = 128
GROUP = 4


def pole_sweep(bases_ref, poles_ref, weight_sq_ref, center, offset, square_only):
    tiles = center.shape[0]

    def block(index, sums):
        base = bases_ref[index]
        relative = poles_ref[pl.ds(index, 1), :] - base
        pole_t = jnp.broadcast_to(relative, (LANES, LANES)).T
        weight_t = jnp.broadcast_to(weight_sq_ref[pl.ds(index, 1), :], (LANES, LANES)).T
        root = (center - base) + offset
        inverse_sums, square_sums = list(sums[0]), list(sums[1])
        for first in range(0, tiles, GROUP):
            members = range(first, min(first + GROUP, tiles))
            points = {m: jnp.broadcast_to(root[m : m + 1, :], (8, LANES)) for m in members}
            part_inverse = {m: None for m in members}
            part_square = {m: None for m in members}
            for k in range(LANES // 8):
                pole = pole_t[8 * k : 8 * k + 8, :]
                weight = weight_t[8 * k : 8 * k + 8, :]
                for m in members:
                    inverse = 1.0 / (pole - points[m])
                    weighted = weight * inverse
                    square = weighted * inverse
                    if k == 0:
                        part_inverse[m], part_square[m] = weighted, square
                    else:
                        part_inverse[m] = part_inverse[m] + weighted
                        part_square[m] = part_square[m] + square
            for m in members:
                inverse_sums[m] = inverse_sums[m] + part_inverse[m]
                square_sums[m] = square_sums[m] + part_square[m]
        if square_only:
            inverse_sums = list(sums[0])
        return tuple(inverse_sums), tuple(square_sums)

    zero = tuple(jnp.zeros((8, LANES), jnp.float32) for _ in range(tiles))
    inverse_sums, square_sums = lax.fori_loop(0, poles_ref.shape[0], block, (zero, zero))
    fold = lambda parts: jnp.concatenate([jnp.sum(p, axis=0, keepdims=True) for p in parts], axis=0)
    return None if square_only else fold(inverse_sums), fold(square_sums)


def roots_kernel(bases_ref, poles_ref, weight_sq_ref, center_ref, offset_ref, left_ref, right_ref, out_ref):
    center = center_ref[...]
    to_left = left_ref[...] - center
    to_right = right_ref[...] - center

    def step(_, offset):
        sum_inverse, sum_square = pole_sweep(bases_ref, poles_ref, weight_sq_ref, center, offset, False)
        limit = 0.5 * jnp.minimum(jnp.abs(to_left - offset), jnp.abs(to_right - offset))
        change = (1.0 + sum_inverse) / sum_square
        return offset - jnp.minimum(jnp.maximum(change, -limit), limit)

    out_ref[...] = lax.fori_loop(0, ITERS, step, offset_ref[...])


def norm_kernel(bases_ref, poles_ref, weight_sq_ref, center_ref, offset_ref, out_ref):
    out_ref[...] = pole_sweep(
        bases_ref, poles_ref, weight_sq_ref, center_ref[...], offset_ref[...], True
    )[1]


def run_kernel(kernel, bases, *operands):
    vmem = pl.BlockSpec(memory_space=pltpu.VMEM)
    return pl.pallas_call(
        kernel,
        out_shape=jax.ShapeDtypeStruct(operands[2].shape, jnp.float32),
        in_specs=[pl.BlockSpec(memory_space=pltpu.SMEM)] + [vmem] * len(operands),
        out_specs=vmem,
    )(bases, *operands)


def lookup(tables, index):
    rows = jnp.concatenate([t.reshape(-1, LANES) for t in tables], axis=1)
    high = lax.reduce_precision(rows, 8, 7)
    middle = lax.reduce_precision(rows - high, 8, 7)
    low = (rows - high) - middle
    pieces = jnp.concatenate([high, middle, low], axis=1).astype(jnp.bfloat16)
    pick = (index[:, None] // LANES == jnp.arange(rows.shape[0])[None, :]).astype(jnp.bfloat16)
    found = jnp.dot(pick, pieces, preferred_element_type=jnp.float32)
    width = rows.shape[1]
    found = (found[:, :width] + found[:, width : 2 * width]) + found[:, 2 * width :]
    lane = index[:, None] % LANES == jnp.arange(LANES)[None, :]
    return [
        jnp.sum(jnp.where(lane, found[:, t * LANES : (t + 1) * LANES], 0.0), axis=1)
        for t in range(len(tables))
    ]


def on_device(pole_values, weights, centers, offsets, chosen, column_pole, eigen_blocks):
    gathered = lax.all_gather(jnp.stack([pole_values, weights]), "row", axis=1, tiled=True)
    all_poles, all_weights = gathered[0], gathered[1]
    rows = lax.axis_size("row")
    per_device = offsets.shape[0] // rows
    first_root = lax.axis_index("row") * per_device
    my_first = lax.axis_index("col") * offsets.shape[0] + first_root
    my_centers = lax.dynamic_slice_in_dim(centers, first_root, per_device)
    my_offsets = lax.dynamic_slice_in_dim(offsets, first_root, per_device)
    shifted = jnp.concatenate([all_poles[1:], all_poles[-1:]])
    left = lax.dynamic_slice_in_dim(all_poles, my_first, per_device)
    right = lax.dynamic_slice_in_dim(shifted, my_first, per_device)

    flat = lambda values: values.reshape(-1, LANES)
    pole_rows = flat(all_poles)
    my_offsets = run_kernel(
        roots_kernel,
        pole_rows[:, LANES // 2],
        pole_rows,
        flat(all_weights * all_weights),
        flat(my_centers),
        flat(my_offsets),
        flat(left),
        flat(right),
    ).reshape(-1)

    match = (chosen[:, None] - my_first) == jnp.arange(per_device)[None, :]
    picked = jnp.stack(
        [
            jnp.sum(jnp.where(match, my_centers[None, :], 0.0), axis=1),
            jnp.sum(jnp.where(match, my_offsets[None, :], 0.0), axis=1),
        ]
    )
    panel_center, panel_offset = lax.psum(picked, ("row", "col"))
    offset_now = lax.all_gather(my_offsets, "row", axis=0, tiled=True)
    local_rows = flat(pole_values)
    partial_sq = run_kernel(
        norm_kernel,
        local_rows[:, LANES // 2],
        local_rows,
        flat(weights * weights),
        flat(panel_center),
        flat(panel_offset),
    ).reshape(-1)
    inv_norm = lax.rsqrt(lax.psum(partial_sq, "row"))

    pole_picked, weight_picked = lookup([all_poles, all_weights], column_pole.reshape(-1))
    pole_picked = pole_picked.reshape(column_pole.shape)
    weight_picked = weight_picked.reshape(column_pole.shape)
    halves = []
    for half in range(column_pole.shape[0]):
        distance = (pole_picked[half][:, None] - panel_center[None, :]) - panel_offset[None, :]
        cauchy = (weight_picked[half][:, None] * (1.0 / distance) * inv_norm[None, :]).astype(jnp.bfloat16)
        part = jnp.dot(eigen_blocks[:, half, :], cauchy, preferred_element_type=jnp.float32)
        sent = part.astype(jnp.bfloat16).reshape(rows, -1, part.shape[1])
        got = lax.all_to_all(sent, "row", split_axis=0, concat_axis=0, tiled=True)
        halves.append(jnp.sum(got.astype(jnp.float32), axis=0))
    return (offset_now, jnp.stack(halves, axis=1))


def solution(mesh):
    placed = (P("row"), P("row"), P("col"), P("col"), P(), P(None, "row"), P("col", None, "row"))
    return jax.shard_map(
        on_device,
        mesh=mesh,
        in_specs=placed,
        out_specs=(P("col"), P(("col", "row"), None, None)),
        check_vma=False,
    )
```

profile of v0, /device:TPU:0, one launch (start us, length us, event | category | flops | bytes accessed | tf_op | source)
XLA Modules:
  0.0 834.3 jit_solution(719434560128669392)
XLA Ops:
  0.6 0.8 pad_maximum_fusion.2
  1.5 33.0 %all_gather.6 = f32[2,65536]{1,0:T(2,128)S(1)} all-gather(f32[2,8192]{1,0:T(2,128)S(1)} %pad_maximum_fusion.2), channel_id=1, replica_groups=mesh['row'=8,'col'=4] {'row'}, dimensions={1}, use_global_device_ids=true | all-gather | bytes 589824 | tf_op jit(solution)/shard_map/all_gather | solution.py:101
  34.5 0.6 slice.85
  35.1 0.6 slice.86
  35.7 0.4 fusion.34
  36.1 0.0 copy-start
  36.1 1.3 dynamic-slice_bitcast_fusion.1.center_ref
  37.5 0.7 dynamic_slice.12
  38.2 1.4 multiply_bitcast_fusion.weight_sq_ref
  39.5 0.8 slice_reduce_fusion.bases_ref
  40.4 0.7 mul.43.weight_sq_ref
  41.1 0.1 reduce-precision_convert_fusion.1
  41.2 0.6 constant_dynamic-slice_fusion
  41.8 0.7 broadcast_subtract_fusion
  42.5 1.9 dynamic-slice_bitcast_fusion
  44.5 0.0 copy-done
  44.5 453.9 %shard_map.86 = f32[16,128]{1,0:T(8,128)} custom-call(f32[512]{0:T(512)} %slice_reduce_fusion.bases_ref, f32[512,128]{1,0:T(8,128)} %bitcast.48, f32[512,128]{1,0:T(8,128)} %mul.43.weight_sq_ref, f32[16,128]{1,0:T(8,128)} %dynamic-slice_bitcast_fusion.1.center_ref, f32[16,128]{1,0:T(8,128)} %get-tuple-element.27.offset_ref, f32[16,128]{1,0:T(8,128)} %bitcast.64, ...), custom_call_target="tpu_custom_call" | custom-call | tf_op jit(solution)/shard_map/pallas_call | solution.py:75
  498.4 6.3 select_reduce_fusion.1
  504.7 39.8 %psum.14 = f32[2,2048]{1,0:T(2,128)S(1)} all-reduce(f32[2,2048]{1,0:T(2,128)S(1)} %pad_maximum_fusion.3), channel_id=1, replica_groups=mesh['row'=8,'col'=4] {'row','col'}, use_global_device_ids=true, to_apply=%region_4.5 | all-reduce | flops 4096 | bytes 32768 | tf_op jit(solution)/shard_map/psum | solution.py:133
  544.5 0.6 fusion.37
  545.1 1.4 slice_reduce_fusion.1.bases_ref
  546.6 17.7 %shard_map.87 = f32[16,128]{1,0:T(8,128)} custom-call(f32[64]{0:T(128)} %slice_reduce_fusion.1.bases_ref, f32[64,128]{1,0:T(8,128)} %bitcast.59, f32[64,128]{1,0:T(8,128)} %multiply_bitcast_fusion.weight_sq_ref, f32[16,128]{1,0:T(8,128)} %bitcast.70, f32[16,128]{1,0:T(8,128)} %bitcast.67), custom_call_target="tpu_custom_call" | custom-call | tf_op jit(solution)/shard_map/pallas_call | solution.py:75
  564.3 20.7 %psum.15 = f32[2048]{0:T(1024)S(1)} all-reduce(f32[2048]{0:T(1024)} %bitcast.66), channel_id=1, replica_groups=mesh['row'=8,'col'=4] {'row'}, use_global_device_ids=true, to_apply=%region_5.6 | all-reduce | flops 2048 | bytes 16384 | tf_op jit(solution)/shard_map/psum | solution.py:144
  585.1 0.6 rsqrt.3
  585.7 0.8 copy.20
  586.5 0.0 slice-start
  586.5 0.0 slice-start.1
  586.5 11.4 %fusion.14 = f32[8192,768]{0,1:T(8,128)} fusion(s32[8192]{0:T(1024)S(1)} %get-tuple-element.24, bf16[512,256]{1,0:T(8,128)(2,1)S(1)} %get-tuple-element.16, bf16[512,256]{1,0:T(8,128)(2,1)S(1)} %get-tuple-element.15, bf16[512,256]{1,0:T(8,128)(2,1)S(1)} %get-tuple-element.14), kind=kOutput, calls=%fused_computation.20 | convolution fusion | flops 6449004544 | bytes 25985024 | tf_op jit(solution)/shard_map/dot_general | solution.py:90
  597.9 0.0 slice-start.2
  597.9 9.0 %slice_add_fusion = f32[8192,256]{0,1:T(8,128)S(1)} fusion(f32[8192,768]{0,1:T(8,128)} %fusion.14), kind=kLoop, calls=%fused_computation.21 | loop fusion | flops 4194304 | bytes 33554432 | tf_op jit(solution)/shard_map/add | solution.py:92
  606.9 0.0 slice-done
  606.9 0.0 slice-done.1
  606.9 0.4 slice-done.2
  607.3 0.0 copy-start.2
  607.3 29.5 %fusion.33 = (bf16[768,1,4096]{2,1,0:T(2,128)(2,1)}, bf16[768,1,4096]{2,1,0:T(2,128)(2,1)}) fusion(bf16[768,2,4096]{2,1,0:T(2,128)(2,1)S(1)} %bitcast.45), kind=kLoop, calls=%fused_computation.69 | loop fusion | bytes 25165824 | tf_op jit(solution)/shard_map/slice | solution.py:153
  636.8 0.9 fusion.17
  637.7 0.0 copy-done.2
  637.7 0.0 copy-start.3
  637.7 0.0 copy-start.4
  637.7 24.2 %fusion.19 = bf16[2048,768]{0,1:T(8,128)(2,1)} fusion(f32[2048]{0:T(1024)} %rsqrt.3, f32[2048]{0:T(1024)S(1)} %bitcast.68, f32[2048]{0:T(1024)} %bitcast.71, f32[4096]{0:T(1024)S(1)} %get-tuple-element.30, f32[4096]{0:T(1024)S(1)} %get-tuple-element.19, bf16[768,1,4096]{2,1,0:T(2,128)(2,1)} %get-tuple-element.12), kind=kOutput, calls=%fused_computation.34 | convolution fusion | flops 12936806400 | bytes 9494528 | tf_op jit(solution)/shard_map/dot_general | solution.py:153
  661.9 3.6 all-to-all-start
  665.6 0.0 copy-done.3
  665.6 0.0 copy-done.4
  665.6 0.0 copy-start.1
  665.6 24.2 %fusion.18 = bf16[2048,768]{0,1:T(8,128)(2,1)} fusion(f32[4096]{0:T(1024)S(1)} %get-tuple-element.29, f32[4096]{0:T(1024)S(1)} %get-tuple-element.20, f32[2048]{0:T(1024)S(1)} %copy-done.4, f32[2048]{0:T(1024)S(1)} %bitcast.69, f32[2048]{0:T(1024)S(1)} %bitcast.72, bf16[768,1,4096]{2,1,0:T(2,128)(2,1)} %get-tuple-element.13), kind=kOutput, calls=%fused_computation.33 | convolution fusion | flops 12936806400 | bytes 9494528 | tf_op jit(solution)/shard_map/dot_general | solution.py:153
  689.8 41.4 %all-to-all-done = bf16[8,96,2048]{2,1,0:T(8,128)(2,1)S(1)} async-done(((bf16[8,96,2048]{2,1,0:T(8,128)(2,1)}), bf16[8,96,2048]{2,1,0:T(8,128)(2,1)S(1)}, u32[]{:S(2)}, u32[]{:S(2)}) %all-to-all-start) | async-done | bytes 3145760 | tf_op jit(solution)/shard_map/all_to_all | solution.py:155
  731.2 4.4 all-to-all-start.1
  735.6 0.0 copy-done.1
  735.6 89.9 %all_gather.7 = f32[16384]{0:T(1024)S(1)} all-gather(f32[2048]{0:T(1024)S(1)} %bitcast.63), channel_id=1, replica_groups=mesh['row'=8,'col'=4] {'row'}, dimensions={0}, use_global_device_ids=true | all-gather | bytes 73728 | tf_op jit(solution)/shard_map/all_gather | solution.py:134
  825.6 1.4 convert_reduce_fusion.1
  827.0 0.0 all-to-all-done.1
  827.0 2.5 convert_reduce_fusion
  829.6 1.2 pad_maximum_fusion
  830.8 2.4 copy.17
  833.2 0.6 copy.30
  (4 shorter events, 0.1 us)
Async XLA Ops:
  36.1 8.3 %copy-start = (f32[1,65536]{1,0:T(1,128)}, f32[1,65536]{1,0:T(1,128)S(1)}, u32[]{:S(2)}) copy-start(f32[1,65536]{1,0:T(1,128)S(1)} %get-tuple-element.18) | copy-start | bytes 786436
  586.5 20.4 %slice-start = ((s8[12582912]{0:T(1024)(128)(4,1)}), s8[4194304]{0:T(1024)(128)(4,1)S(1)}, s32[]{:S(2)}) async-start(s8[12582912]{0:T(1024)(128)(4,1)} %bitcast.44), calls=%async_computation.2 | async-start | bytes 8388608
  586.5 20.4 %slice-start.1 = ((s8[12582912]{0:T(1024)(128)(4,1)}), s8[4194304]{0:T(1024)(128)(4,1)S(1)}, s32[]{:S(2)}) async-start(s8[12582912]{0:T(1024)(128)(4,1)} %bitcast.44), calls=%async_computation.3 | async-start | bytes 8388608
  597.9 9.4 %slice-start.2 = ((s8[12582912]{0:T(1024)(128)(4,1)}), s8[4194304]{0:T(1024)(128)(4,1)S(1)}, s32[]{:S(2)}) async-start(s8[12582912]{0:T(1024)(128)(4,1)} %bitcast.44), calls=%async_computation.4 | async-start | bytes 8388608
  607.3 30.4 %copy-start.2 = (f32[1,2048]{1,0:T(1,128)S(1)}, f32[1,2048]{1,0:T(1,128)}, u32[]{:S(2)}) copy-start(f32[1,2048]{1,0:T(1,128)} %get-tuple-element.25) | copy-start | bytes 24580
  637.7 27.9 %copy-start.3 = (f32[1,2048]{1,0:T(1,128)S(1)}, f32[1,2048]{1,0:T(1,128)}, u32[]{:S(2)}) copy-start(f32[1,2048]{1,0:T(1,128)} %get-tuple-element.26) | copy-start | bytes 24580
  637.7 27.9 %copy-start.4 = (f32[2048]{0:T(1024)S(1)}, f32[2048]{0:T(1024)}, u32[]{:S(2)}) copy-start(f32[2048]{0:T(1024)} %rsqrt.3) | copy-start | bytes 24580
  661.9 69.3 %all-to-all-start = ((bf16[8,96,2048]{2,1,0:T(8,128)(2,1)}), bf16[8,96,2048]{2,1,0:T(8,128)(2,1)S(1)}, u32[]{:S(2)}, u32[]{:S(2)}) async-start(bf16[8,96,2048]{2,1,0:T(8,128)(2,1)} %bitcast.53), calls=%async_computation | async-start | bytes 6291456 | tf_op jit(solution)/shard_map/all_to_all | solution.py:155
  665.6 70.0 %copy-start.1 = (f32[16,128]{1,0:T(8,128)S(1)}, f32[16,128]{1,0:T(8,128)}, u32[]{:S(2)}) copy-start(f32[16,128]{1,0:T(8,128)} %shard_map.86) | copy-start | bytes 24580
  731.2 95.8 %all-to-all-start.1 = ((bf16[8,96,2048]{2,1,0:T(8,128)(2,1)}), bf16[8,96,2048]{2,1,0:T(8,128)(2,1)}, u32[]{:S(2)}, u32[]{:S(2)}) async-start(bf16[8,96,2048]{2,1,0:T(8,128)(2,1)} %bitcast.52), calls=%async_computation.1 | async-start | bytes 6291456 | tf_op jit(solution)/shard_map/all_to_all | solution.py:155
where the time goes:
time: 841 us; the launch traced here: 834 us
  Pallas kernels  472 us (56%)
  blocking collectives  184 us (22%)
  matrix products  59.7 us (7%)
  local copies, waits for them, and re-layouts  41.4 us (5%)
  waiting for transfers between devices  41.4 us (5%)
  other arithmetic  27.2 us (3%)
    pallas_call x2, Pallas kernels, run_kernel(): pl.pallas_call(kernel, out_shape=jax.ShapeDtypeStruct(operands[2].shape,...  472 us
    all_gather x1, blocking collectives, on_device(): offset_now = lax.all_gather(my_offsets, 'row', axis=0, tiled=True)  89.9 us
    dot_general x2, matrix products, on_device(): jnp.dot(eigen_blocks[:, half, :], cauchy, preferred_element_type=jnp.floa...  48.4 us
    all_to_all x2, waiting for transfers between devices, on_device(): got = lax.all_to_all(sent, 'row', split_axis=0, concat_axis=0, tiled=True)  41.4 us
    psum x1, blocking collectives, on_device(): panel_center, panel_offset = lax.psum(picked, ('row', 'col'))  39.8 us
    all_gather x1, blocking collectives, on_device(): lax.all_gather(jnp.stack([pole_values, weights]), 'row', axis=1, tiled=True)  33 us
    slice x1, local copies, waits for them, and re-layouts, on_device(): eigen_blocks[:, half, :]  29.5 us
    psum x1, blocking collectives, on_device(): inv_norm = lax.rsqrt(lax.psum(partial_sq, 'row'))  20.7 us
  transfers between devices with their start and end apart: 2, of which 1 were waited for; matrix products, arithmetic and copies ran while one was open for 3% of the time, Pallas kernels for 0%

commit v1 on v0

v1 whole, which is shorter than its diff:
```python
import itertools
import jax
import jax.numpy as jnp
from jax import lax
from jax.experimental import pallas as pl
from jax.experimental.pallas import tpu as pltpu
from jax.sharding import PartitionSpec as P

AXES = ("row", "col")
LANES = 128
ITERS = 3
BLOCK = 32
TERMS = 40
KAPPA = 8.0
PAIR = 2
PIECES = 3
WIDTH = 256
DEPTH = 1024
PARTS = 2
FLOPS_PER_US = 1_000_000_000


def power(base, exponent):
    result = jnp.ones_like(base)
    square = base
    for bit in range(6):
        result = jnp.where((exponent >> bit) & 1 == 1, result * square, result)
        square = square * square
    return result


def pieces(values):
    high = values.astype(jnp.bfloat16).astype(jnp.float32)
    return high, values - high


def gather(items, collective_id):
    sizes = {axis: lax.axis_size(axis) for axis in AXES}
    offsets_of = lambda axes: list(itertools.product(*[range(sizes[a]) if a in axes else (0,) for a in AXES]))
    groups = [offsets_of(axes) for _, axes in items]
    greeted = sorted({offset for group in groups for offset in group[1:]})
    count = len(items)

    def kernel(*refs):
        sources, targets, send, receive = refs[:count], refs[count : 2 * count], refs[2 * count], refs[2 * count + 1]
        here = [lax.axis_index(axis) for axis in AXES]
        device = lambda offset: tuple(lax.rem(h + o, sizes[a]) for h, o, a in zip(here, offset, AXES))
        barrier = pltpu.get_barrier_semaphore()
        for offset in greeted:
            pl.semaphore_signal(barrier, inc=1, device_id=device(offset), device_id_type=pl.DeviceIdType.MESH)
        pl.semaphore_wait(barrier, len(greeted))
        copies = []
        for (_, axes), group, source, target in zip(items, groups, sources, targets):
            slot = 0
            for h, a in zip(here, AXES):
                if a in axes:
                    slot = slot * sizes[a] + h
            for offset in group[1:]:
                copies.append(
                    pltpu.make_async_remote_copy(
                        src_ref=source,
                        dst_ref=target.at[slot],
                        send_sem=send.at[len(copies)],
                        recv_sem=receive.at[len(copies)],
                        device_id=device(offset),
                        device_id_type=pl.DeviceIdType.MESH,
                    )
                )
                copies[-1].start()
            target[slot] = source[...]
        for copy in copies:
            copy.wait()

    total = sum(len(group) - 1 for group in groups)
    vmem = pl.BlockSpec(memory_space=pltpu.VMEM)
    return pl.pallas_call(
        kernel,
        out_shape=[jax.ShapeDtypeStruct((len(g),) + v.shape, v.dtype) for (v, _), g in zip(items, groups)],
        in_specs=[vmem] * count,
        out_specs=[vmem] * count,
        scratch_shapes=[pltpu.SemaphoreType.DMA((total,)), pltpu.SemaphoreType.DMA((total,))],
        compiler_params=pltpu.CompilerParams(collective_id=collective_id, has_side_effects=True),
        name="gather",
    )(*[v for v, _ in items])


def coefficients_kernel(geometry_ref, block_poles_ref, block_weights_ref, *refs):
    coeff_ref, top_ref, bottom_ref = refs[-3:]
    q = pl.program_id(1)
    blank = jnp.zeros((8, LANES), jnp.float32)
    for k in range(BLOCK, TERMS):
        top_ref[8 * k : 8 * k + 8, :] = blank
        bottom_ref[8 * k : 8 * k + 8, :] = blank
    middle, radius, first, last = (geometry_ref[i] for i in range(4))
    inverse_radius = 1.0 / radius
    block = (q * LANES + lax.broadcasted_iota(jnp.int32, (8, LANES), 1)).astype(jnp.float32)
    far = jnp.logical_or(block < first, block >= last)
    scale = jnp.where(far, radius, 0.0)
    top, bottom = [], [jnp.ones((8, LANES), jnp.float32)]
    for j in range(BLOCK):
        weight = block_weights_ref[0, j : j + 1, :]
        ratio = scale / (block_poles_ref[0, j : j + 1, :] - middle)
        value = (weight * weight) * ratio * inverse_radius
        new_top, new_bottom = [], []
        for k in range(j + 1):
            term = value * bottom[k]
            if k < j:
                term = top[k] + term
            if k > 0:
                term = term - ratio * top[k - 1]
            new_top.append(term)
        for k in range(j + 2):
            term = bottom[k] if k <= j else None
            if k > 0:
                shifted = ratio * bottom[k - 1]
                term = -shifted if term is None else term - shifted
            new_bottom.append(term)
        top, bottom = new_top, new_bottom
    for k in range(BLOCK):
        top_ref[8 * k : 8 * k + 8, :] = top[k]
    for k in range(BLOCK + 1):
        bottom_ref[8 * k : 8 * k + 8, :] = bottom[k]
    for member in range(coeff_ref.shape[0]):
        for ref, at in ((top_ref, 0), (bottom_ref, LANES)):
            high, low = pieces(ref[pl.ds(member, TERMS, stride=8), :])
            rows = jnp.concatenate([high, low, high, blank], axis=0)
            coeff_ref[member, 0, :, at : at + LANES] = rows.astype(jnp.bfloat16)


def update_kernel(near_ref, middle_ref, radius_ref, first_ref, poles_ref, weights_ref, center_ref, offset_ref, coeff_ref, *refs):
    out_ref = refs[-1]
    tile = pl.program_id(0)
    chunks = coeff_ref.shape[1]
    order = lax.broadcasted_iota(jnp.int32, (TERMS, LANES), 0)
    blank = jnp.zeros((8, LANES), jnp.float32)

    def to_rows(values):
        high, low = pieces(values)
        return jnp.concatenate([high, high, low, blank], axis=0).T.astype(jnp.bfloat16)

    center, offset = center_ref[0], offset_ref[0]
    middle, radius = middle_ref[tile], radius_ref[tile]
    place = (center - middle) + offset
    ratio = jnp.broadcast_to(place / radius, (TERMS, LANES))
    value_rows = to_rows(power(ratio, order))
    slope_rows = to_rows(order.astype(jnp.float32) * power(ratio, jnp.maximum(order - 1, 0)))
    rows = jnp.concatenate([value_rows, slope_rows], axis=0)
    inverse_sum = square_sum = None
    for q in range(chunks):
        got = jnp.dot(rows, coeff_ref[0, q], preferred_element_type=jnp.float32)
        top, bottom = got[:LANES, :LANES], got[:LANES, LANES:]
        top_slope, bottom_slope = got[LANES:, :LANES], got[LANES:, LANES:]
        inverse = 1.0 / bottom
        quotient = top * inverse
        slope = (top_slope - quotient * bottom_slope) * inverse
        inverse_sum = quotient if q == 0 else inverse_sum + quotient
        square_sum = slope if q == 0 else square_sum + slope
    square_sum = square_sum / radius
    place_rows = jnp.broadcast_to(place, (LANES, LANES)).T
    inverse_parts, square_parts = [], []
    half = LANES // 2
    for part in range(2):
        own = slice(part * half, (part + 1) * half)
        points = place_rows[own]

        def near(step, sums):
            inverse_sum, square_sum = sums
            for i in range(PAIR):
                row = step * PAIR + i
                pole = poles_ref[pl.ds(row, 1), :] - middle
                weight = weights_ref[pl.ds(row, 1), :]
                inverse = 1.0 / (pole - points)
                weighted = (weight * weight) * inverse
                inverse_sum = inverse_sum + weighted
                square_sum = square_sum + weighted * inverse
            return inverse_sum, square_sum

        sums = lax.fori_loop(near_ref[0, tile], near_ref[1, tile], near, (inverse_sum[own], square_sum[own]))
        inverse_parts.append(sums[0])
        square_parts.append(sums[1])
    total = lambda parts: jnp.sum(jnp.concatenate(parts, axis=0).T, axis=0, keepdims=True)
    sum_inverse, sum_square = total(inverse_parts), total(square_parts)
    row = first_ref[0] + tile
    to_left = poles_ref[pl.ds(row, 1), :] - center
    final = lax.broadcasted_iota(jnp.int32, (1, LANES), 1) + row * LANES == poles_ref.shape[0] * LANES - 1
    to_right = jnp.where(final, to_left, -to_left)
    limit = 0.5 * jnp.minimum(jnp.abs(to_left - offset), jnp.abs(to_right - offset))
    change = (1.0 + sum_inverse) / sum_square
    out_ref[0] = offset - jnp.minimum(jnp.maximum(change, -limit), limit)


def find_roots(poles, weights, centers, offsets, my_first, after):
    flat = lambda values: values.reshape(-1, LANES)
    tiles = centers.shape[0] // LANES
    chunks = poles.shape[0] // (BLOCK * LANES)
    tile_centers = flat(centers)
    middle = tile_centers[:, LANES // 2]
    radius = jnp.maximum(tile_centers[:, -1] - middle, middle - tile_centers[:, 0]) + 2.5
    below = jnp.sum((poles[None, :] <= (middle - KAPPA * radius)[:, None]).astype(jnp.int32), axis=1)
    inside = jnp.sum((poles[None, :] < (middle + KAPPA * radius)[:, None]).astype(jnp.int32), axis=1)
    unit = PAIR * LANES
    near = jnp.stack([below // unit, (inside + unit - 1) // unit])
    limits = (near * (unit // BLOCK)).astype(jnp.float32)
    octet = min(tiles, 8)
    geometry = jnp.stack([middle, radius, limits[0], limits[1]])
    geometry = jnp.pad(geometry, ((0, 0), (0, -tiles % 8)), mode="edge")
    geometry = jnp.broadcast_to(geometry[:, :, None], geometry.shape + (LANES,))
    blocked = lambda values: values.reshape(chunks, LANES, BLOCK).transpose(0, 2, 1)
    smem, anywhere = pl.BlockSpec(memory_space=pltpu.SMEM), pl.BlockSpec(memory_space=pl.ANY)
    coeff = pl.pallas_call(
        coefficients_kernel,
        grid=(geometry.shape[1] // 8, chunks),
        out_shape=jax.ShapeDtypeStruct((tiles, chunks, LANES, 2 * LANES), jnp.bfloat16),
        in_specs=[
            pl.BlockSpec((4, 8, LANES), lambda o, q: (0, o, 0)),
            pl.BlockSpec((1, BLOCK, LANES), lambda o, q: (q, 0, 0)),
            pl.BlockSpec((1, BLOCK, LANES), lambda o, q: (q, 0, 0)),
        ] + [anywhere] * len(after[0]),
        out_specs=pl.BlockSpec((octet, 1, LANES, 2 * LANES), lambda o, q: (o, q, 0, 0)),
        scratch_shapes=[pltpu.VMEM((8 * TERMS, LANES), jnp.float32)] * 2,
        cost_estimate=pl.CostEstimate(flops=FLOPS_PER_US * 18, bytes_accessed=tiles * chunks * LANES * LANES * 4, transcendentals=0),
        name="coefficients",
    )(geometry, blocked(poles), blocked(weights), *after[0])
    whole = pl.BlockSpec((poles.shape[0] // LANES, LANES), lambda t: (0, 0))
    one = pl.BlockSpec((1, 1, LANES), lambda t: (t, 0, 0))
    spread = lambda values: values.reshape(tiles, 1, LANES)
    now = spread(offsets)
    first = (my_first // LANES).reshape(1)
    for step in range(ITERS):
        now = pl.pallas_call(
            update_kernel,
            grid=(tiles,),
            out_shape=jax.ShapeDtypeStruct((tiles, 1, LANES), jnp.float32),
            in_specs=[smem] * 4 + [whole] * 2 + [one] * 2 + [pl.BlockSpec((1, chunks, LANES, 2 * LANES), lambda t: (t, 0, 0, 0))] + [anywhere] * len(after[step + 1]),
            out_specs=one,
            cost_estimate=pl.CostEstimate(flops=FLOPS_PER_US * 18, bytes_accessed=tiles * chunks * LANES * LANES * 4, transcendentals=0),
            name="update",
        )(near, middle, radius, first, flat(poles), flat(weights), spread(centers), now, coeff, *after[step + 1])
    return now.reshape(-1)


def lookup_kernel(index_ref, *refs):
    count = (len(refs) - 1) // 2
    tables, targets, pieces_ref = refs[:count], refs[count : 2 * count], refs[2 * count]
    rows = tables[0].shape[0]

    @pl.when(pl.program_id(0) == 0)
    def _():
        for t, table in enumerate(tables):
            rest = table[...]
            for p in range(PIECES):
                part = rest.astype(jnp.bfloat16)
                at = (t * PIECES + p) * LANES
                pieces_ref[:, at : at + LANES] = part
                rest = rest - part.astype(jnp.float32)

    lane = lax.broadcasted_iota(jnp.int32, (LANES, LANES), 1)
    for g in range(index_ref.shape[0]):
        index = jnp.broadcast_to(index_ref[g], (LANES, LANES)).T
        high = lax.shift_right_logical(index, 7)
        low = lax.bitwise_and(index, LANES - 1)
        pick = jnp.concatenate([(high == lane + c * LANES).astype(jnp.float32) for c in range(rows // LANES)], axis=1)
        found = jnp.dot(pick.astype(jnp.bfloat16), pieces_ref[...], preferred_element_type=jnp.float32)
        for t, target in enumerate(targets):
            parts = [found[:, (t * PIECES + p) * LANES : (t * PIECES + p + 1) * LANES] for p in range(PIECES)]
            value = (parts[0] + parts[1]) + parts[2]
            value = jnp.sum(jnp.where(low == lane, value, 0.0), axis=1, keepdims=True)
            target[g * LANES : (g + 1) * LANES, :] = jnp.broadcast_to(value, (LANES, LANES))


def lookup(tables, index):
    groups = index.shape[0] // LANES
    step = min(groups, 8)
    count = len(tables)
    return pl.pallas_call(
        lookup_kernel,
        grid=(groups // step,),
        out_shape=[jax.ShapeDtypeStruct((index.shape[0], LANES), jnp.float32)] * count,
        in_specs=[pl.BlockSpec((step, 1, LANES), lambda i: (i, 0, 0))] + [pl.BlockSpec(t.shape, lambda i: (0, 0)) for t in tables],
        out_specs=[pl.BlockSpec((step * LANES, LANES), lambda i: (i, 0))] * count,
        scratch_shapes=[pltpu.VMEM((tables[0].shape[0], count * PIECES * LANES), jnp.bfloat16)],
        name="lookup",
    )(index.reshape(groups, 1, LANES), *tables)


def chosen_kernel(poles_ref, weights_ref, last_ref, left_ref, right_ref, start_ref, out_ref):
    count = last_ref.shape[0]
    left, right = left_ref[:count], right_ref[:count]
    center = jnp.where(last_ref[...] > 0, left + 0.5, 0.5 * (left + right))
    to_left, to_right = left - center, right - center
    rows = poles_ref.shape[0]

    def sweep(offset, square_only):
        def row(index, sums):
            inverse = 1.0 / ((poles_ref[pl.ds(index, 1), :] - center) - offset)
            weight = weights_ref[pl.ds(index, 1), :]
            weighted = (weight * weight) * inverse
            square_sum = sums[1] + weighted * inverse
            return (sums[0] if square_only else sums[0] + weighted), square_sum

        zero = jnp.zeros_like(center)
        sums = lax.fori_loop(0, rows, row, (zero, zero), unroll=8)
        return [jnp.broadcast_to(jnp.sum(s, axis=1, keepdims=True), center.shape) for s in sums]

    def step(_, offset):
        sum_inverse, sum_square = sweep(offset, False)
        limit = 0.5 * jnp.minimum(jnp.abs(to_left - offset), jnp.abs(to_right - offset))
        change = (1.0 + sum_inverse) / sum_square
        return offset - jnp.minimum(jnp.maximum(change, -limit), limit)

    offset = lax.fori_loop(0, ITERS, step, start_ref[:count])
    norm = lax.rsqrt(sweep(offset, True)[1])
    lane = lax.broadcasted_iota(jnp.int32, (count, LANES), 1)
    own = lane == lax.broadcasted_iota(jnp.int32, (count, LANES), 0)
    spread = lambda values: jnp.sum(jnp.where(own, values, 0.0), axis=0, keepdims=True)
    blank = jnp.zeros((5, LANES), jnp.float32)
    out_ref[...] = jnp.concatenate([spread(center), spread(offset), spread(norm), blank], axis=0)


def panel_kernel(side_ref, pole_ref, weight_ref, center_ref, offset_ref, norm_ref, eigen_ref, send_ref, keep_ref, total_ref):
    depth = eigen_ref.shape[2]
    center, offset, norm = center_ref[...], offset_ref[...], norm_ref[...]
    total = None
    for first in range(0, depth, DEPTH):
        rows = slice(first, first + DEPTH)
        columns = []
        for at in range(0, WIDTH, LANES):
            lanes = slice(at, at + LANES)
            distance = (pole_ref[rows, :] - center[:, lanes]) - offset[:, lanes]
            columns.append((weight_ref[rows, :] * (1.0 / distance) * norm[:, lanes]).astype(jnp.bfloat16))
        part = jnp.dot(eigen_ref[0, :, rows], jnp.concatenate(columns, axis=1), preferred_element_type=jnp.float32)
        total = part if total is None else total + part
    total_ref[...] = total
    side = side_ref[0]
    size = send_ref.shape[1]
    for z in range(send_ref.shape[0]):
        send_ref[z] = total_ref[pl.ds(pl.multiple_of((2 * z + 1 - side) * size, 8), size), :].astype(jnp.bfloat16)
        keep_ref[z] = total_ref[pl.ds(pl.multiple_of((2 * z + side) * size, 8), size), :]


def panel_part(side, pole, weight, panel, eigen, half, first, width, rows):
    height, depth = eigen.shape[1], eigen.shape[2]
    shape = (rows // 2, height // rows, width)
    row = pl.BlockSpec((1, WIDTH), lambda i: (0, first // WIDTH + i))
    wide = pl.BlockSpec((depth, LANES), lambda i: (half, 0))
    out = pl.BlockSpec(shape[:2] + (WIDTH,), lambda i: (0, 0, i))
    return pl.pallas_call(
        panel_kernel,
        grid=(width // WIDTH,),
        out_shape=[jax.ShapeDtypeStruct(shape, jnp.bfloat16), jax.ShapeDtypeStruct(shape, jnp.float32)],
        in_specs=[pl.BlockSpec(memory_space=pltpu.SMEM), wide, wide, row, row, row, pl.BlockSpec((1, height, depth), lambda i: (half, 0, 0))],
        out_specs=[out, out],
        scratch_shapes=[pltpu.VMEM((height, WIDTH), jnp.float32)],
        cost_estimate=pl.CostEstimate(flops=FLOPS_PER_US * 9, bytes_accessed=height * depth * 2, transcendentals=0),
        compiler_params=pltpu.CompilerParams(vmem_limit_bytes=56 * 1024 * 1024),
        name="panel",
    )(side, pole, weight, *[p[None, :] for p in panel], eigen)


def on_device(pole_values, weights, centers, offsets, chosen, column_pole, eigen_blocks):
    flat = lambda values: values.reshape(-1, LANES)
    rows, cols = lax.axis_size("row"), lax.axis_size("col")
    row, col = lax.axis_index("row"), lax.axis_index("col")
    per_device = offsets.shape[0] // rows
    first_root = row * per_device
    my_first = col * offsets.shape[0] + first_root
    all_poles, all_weights, all_offsets = gather_inputs(pole_values, weights, offsets)
    total = all_poles.shape[0]

    share = chosen.shape[0] // (rows * cols)
    mine = lax.dynamic_slice_in_dim(chosen, (row * cols + col) * share, share)
    padded = jnp.pad(mine, (0, LANES - share))
    index = jnp.concatenate([padded, jnp.minimum(padded + 1, total - 1)])
    found_pole, found_offset = lookup([flat(all_poles), flat(all_offsets)], index)
    last = jnp.broadcast_to((mine == total - 1).astype(jnp.int32)[:, None], (share, LANES))
    here = pl.BlockSpec(memory_space=pltpu.VMEM)
    packed = pl.pallas_call(
        chosen_kernel, out_shape=jax.ShapeDtypeStruct((8, LANES), jnp.float32), in_specs=[here] * 6, out_specs=here, name="chosen"
    )(flat(all_poles), flat(all_weights), last, found_pole[:LANES], found_pole[LANES:], found_offset[:LANES])
    panel = gather([(packed, AXES)], 1)[0][:, :3, :share].transpose(1, 0, 2).reshape(3, -1)

    pole, weight = lookup([flat(all_poles), flat(all_weights)], column_pole.reshape(-1))
    eigen = jnp.transpose(eigen_blocks, (1, 0, 2))
    side = lax.rem(row, 2).reshape(1)
    deep = row // 2
    near_pairs = [(r, r ^ 1) for r in range(rows)]
    received, outgoing = [], []
    width = chosen.shape[0] // PARTS
    for half in range(column_pole.shape[0]):
        for first in range(0, chosen.shape[0], width):
            send, keep = panel_part(side, pole, weight, panel, eigen, half, first, width, rows)
            met = lax.ppermute(send, "row", near_pairs)
            both = keep + met.astype(jnp.float32)
            blocks, arrived = [], [lax.dynamic_index_in_dim(both, deep, 0, keepdims=False)]
            for shift in range(1, rows // 2):
                block = lax.dynamic_index_in_dim(both, lax.rem(deep + shift, rows // 2), 0, keepdims=False)
                blocks.append(block.astype(jnp.bfloat16))
                pairs = [(r, (r + 2 * shift) % rows) for r in range(rows)]
                arrived.append(lax.ppermute(blocks[-1], "row", pairs))
            outgoing.append(blocks)
            received.append(arrived)

    my_centers = lax.dynamic_slice_in_dim(centers, first_root, per_device)
    my_offsets = lax.dynamic_slice_in_dim(offsets, first_root, per_device)
    after = [outgoing[0] + outgoing[1], outgoing[2], outgoing[3], []]
    my_offsets = find_roots(all_poles, all_weights, my_centers, my_offsets, my_first, after)
    offset_now = gather([(flat(my_offsets), ("row",))], 2)[0].reshape(-1)
    add = lambda parts: sum([p.astype(jnp.float32) for p in parts[1:]], parts[0])
    halves = [jnp.concatenate([add(parts) for parts in received[at : at + PARTS]], axis=1) for at in range(0, len(received), PARTS)]
    return (offset_now, jnp.stack(halves, axis=1))


def gather_inputs(pole_values, weights, offsets):
    flat = lambda values: values.reshape(-1, LANES)
    all_poles, all_weights, all_offsets = gather([(flat(pole_values), ("row",)), (flat(weights), ("row",)), (flat(offsets), ("col",))], 0)
    return all_poles.reshape(-1), all_weights.reshape(-1), all_offsets.reshape(-1)


def solution(mesh):
    placed = (P("row"), P("row"), P("col"), P("col"), P(), P(None, "row"), P("col", None, "row"))

    return jax.shard_map(
        on_device,
        mesh=mesh,
        in_specs=placed,
        out_specs=(P("col"), P(("col", "row"), None, None)),
        check_vma=False,
    )
```

time: 841 us -> 314 us (0.37)
  Pallas kernels: 472 us -> 209 us
  blocking collectives: 184 us -> 0 us
  matrix products: 59.7 us -> 0 us
  starting transfers between devices: 8.09 us -> 24.3 us
  other arithmetic: 27.2 us -> 13.1 us
  waiting for transfers between devices: 41.4 us -> 28 us
    pallas_call x2 -> x14, Pallas kernels: 472 us -> 209 us  [the longest x3 62.6 us: find_roots(): pl.pallas_call(update_kernel, grid=(tiles,), out_shape=jax.ShapeDtypeStru...]
    all_gather x2 -> x0, blocking collectives: 123 us -> none  [the longest x1 89.9 us: on_device(): offset_now = lax.all_gather(my_offsets, 'row', axis=0, tiled=True)]
    psum x2 -> x0, blocking collectives: 60.5 us -> none  [the longest x1 39.8 us: on_device(): panel_center, panel_offset = lax.psum(picked, ('row', 'col'))]
    dot_general x3 -> x0, matrix products: 59.7 us -> none  [the longest x2 48.4 us: on_device(): jnp.dot(eigen_blocks[:, half, :], cauchy, preferred_element_type=jnp.floa...]
    all_to_all x2 -> x0, waiting for transfers between devices: 41.4 us -> none  [on_device(): got = lax.all_to_all(sent, 'row', split_axis=0, concat_axis=0, tiled=True)]
    slice x7 -> x2, local copies, waits for them, and re-layouts: 33.4 us -> 3 us  [the longest x1 1.53 us: on_device(): found_pole[LANES:]]
    ppermute x0 -> x16, waiting for transfers between devices: none -> 28 us  [the longest x12 21.5 us: on_device(): arrived.append(lax.ppermute(blocks[-1], 'row', pairs))]
    ppermute x0 -> x16, starting transfers between devices: none -> 24.3 us  [the longest x12 20.2 us: on_device(): arrived.append(lax.ppermute(blocks[-1], 'row', pairs))]
  transfers between devices with their start and end apart: 2 -> 16, of which waited for: 1 -> 4; matrix products, arithmetic and copies ran while one was open for 3% -> 7% of each run, Pallas kernels for 0% -> 43%
where the time goes in v1:
time: 314 us; the launch traced here: 310 us
  Pallas kernels  209 us (67%)
  local copies, waits for them, and re-layouts  35.1 us (11%)
  waiting for transfers between devices  28 us (9%)
  starting transfers between devices  24.3 us (8%)
  other arithmetic  13.1 us (4%)
    pallas_call x3, Pallas kernels, find_roots(): pl.pallas_call(update_kernel, grid=(tiles,), out_shape=jax.ShapeDtypeStru...  62.6 us
    pallas_call x4, Pallas kernels, panel_part(): pl.pallas_call(panel_kernel, grid=(width // WIDTH,), out_shape=[jax.Shape...  50.7 us
    pallas_call x3, Pallas kernels, gather(): pl.pallas_call(kernel, out_shape=[jax.ShapeDtypeStruct((len(g),) + v.shap...  38.8 us
    pallas_call x1, Pallas kernels, find_roots(): pl.pallas_call(coefficients_kernel, grid=(geometry.shape[1] // 8, chunks)...  24.5 us
    ppermute x12, waiting for transfers between devices, on_device(): arrived.append(lax.ppermute(blocks[-1], 'row', pairs))  21.5 us
    ppermute x12, starting transfers between devices, on_device(): arrived.append(lax.ppermute(blocks[-1], 'row', pairs))  20.2 us
    pallas_call x1, Pallas kernels, on_device(): pl.pallas_call(chosen_kernel, out_shape=jax.ShapeDtypeStruct((8, LANES),...  18.6 us
    unnamed x29, local copies, waits for them, and re-layouts  17.5 us
  transfers between devices with their start and end apart: 16, of which 4 were waited for; matrix products, arithmetic and copies ran while one was open for 7% of the time, Pallas kernels for 43%

profile of v1, /device:TPU:0, one launch (start us, length us, event | category | flops | bytes accessed | tf_op | source)
XLA Modules:
  0.0 310.1 jit_solution(1748081703631170955)
XLA Ops:
  0.6 0.8 compare_convert_fusion
  1.4 0.6 pad_add_fusion.1.index_ref
  2.0 19.3 %gather.3 = (f32[8,64,128]{2,1,0:T(8,128)}, f32[8,64,128]{2,1,0:T(8,128)}, f32[4,128,128]{2,1,0:T(8,128)}) custom-call(f32[64,128]{1,0:T(8,128)} %bitcast.127, f32[64,128]{1,0:T(8,128)} %bitcast.128, f32[128,128]{1,0:T(8,128)} %bitcast.126), custom_call_target="tpu_custom_call" | custom-call | tf_op jit(solution)/shard_map/gather/pallas_call | solution.py:76
  21.3 2.3 lookup.3
  23.6 1.5 fusion.22
  25.1 1.5 slice.32.start_ref
  26.6 0.7 broadcast_in_dim.5.last_ref
  27.3 18.6 %chosen.1.refs_0_ = f32[8,128]{1,0:T(8,128)} custom-call(f32[512,128]{1,0:T(8,128)} %bitcast.111, f32[512,128]{1,0:T(8,128)} %bitcast.117, s32[64,128]{1,0:T(8,128)} %broadcast_in_dim.5.last_ref, f32[128,128]{1,0:T(8,128)} %get-tuple-element.65.left_ref, f32[128,128]{1,0:T(8,128)} %get-tuple-element.64.right_ref, f32[128,128]{1,0:T(8,128)} %slice.32.start_ref), custom_call_target="tpu_custom_call" | custom-call | tf_op jit(solution)/shard_map/chosen/pallas_call | solution.py:377
  45.9 10.6 %gather.4 = f32[32,8,128]{2,1,0:T(8,128)} custom-call(f32[8,128]{1,0:T(8,128)} %chosen.1.refs_0_), custom_call_target="tpu_custom_call" | custom-call | tf_op jit(solution)/shard_map/gather/pallas_call | solution.py:76
  56.5 0.9 slice_bitcast_fusion
  57.6 0.7 unstack.25.center_ref
  58.3 0.7 unstack.27.offset_ref
  58.9 0.7 unstack.29.norm_ref
  59.6 0.7 reshape_reshape.34.index_ref
  60.3 11.3 %lookup.2 = (f32[8192,128]{1,0:T(8,128)}, f32[8192,128]{1,0:T(8,128)}) custom-call(s32[64,1,128]{2,1,0:T(1,128)} %reshape_reshape.34.index_ref, f32[512,128]{1,0:T(8,128)} %bitcast.112, f32[512,128]{1,0:T(8,128)} %bitcast.118), custom_call_target="tpu_custom_call" | custom-call | tf_op jit(solution)/shard_map/lookup/pallas_call | solution.py:275
  71.5 14.5 %copy.24 = bf16[768,2,4096]{2,0,1:T(8,128)(2,1)} copy(bf16[768,2,4096]{2,1,0:T(2,128)(2,1)} %param.13) | data formatting | bytes 25165824 | tf_op args[6]
  86.0 12.6 %panel.4 = (bf16[4,96,1024]{2,1,0:T(8,128)(2,1)}, f32[4,96,1024]{2,1,0:T(8,128)}) custom-call(s32[1]{0:T(128)} %bitcast.14.side_ref, f32[8192,128]{1,0:T(8,128)} %get-tuple-element.19.pole_ref, f32[8192,128]{1,0:T(8,128)} %get-tuple-element.20.weight_ref, f32[1,2048]{1,0:T(1,128)} %unstack.25.center_ref, f32[1,2048]{1,0:T(1,128)} %unstack.27.offset_ref, ...), custom_call_target="tpu_custom_call" | custom-call | flops 8999999488 | bytes 6291456 | tf_op jit(solution)/shard_map/panel/pallas_call | solution.py:347
  98.7 1.8 collective-permute-start
  100.4 12.7 %panel.5 = (bf16[4,96,1024]{2,1,0:T(8,128)(2,1)}, f32[4,96,1024]{2,1,0:T(8,128)}) custom-call(s32[1]{0:T(128)} %bitcast.14.side_ref, f32[8192,128]{1,0:T(8,128)} %get-tuple-element.19.pole_ref, f32[8192,128]{1,0:T(8,128)} %get-tuple-element.20.weight_ref, f32[1,2048]{1,0:T(1,128)} %unstack.25.center_ref, f32[1,2048]{1,0:T(1,128)} %unstack.27.offset_ref, ...), custom_call_target="tpu_custom_call" | custom-call | flops 8999999488 | bytes 6291456 | tf_op jit(solution)/shard_map/panel/pallas_call | solution.py:347
  113.4 12.7 %panel.6 = (bf16[4,96,1024]{2,1,0:T(8,128)(2,1)}, f32[4,96,1024]{2,1,0:T(8,128)}) custom-call(s32[1]{0:T(128)} %bitcast.14.side_ref, f32[8192,128]{1,0:T(8,128)} %get-tuple-element.19.pole_ref, f32[8192,128]{1,0:T(8,128)} %get-tuple-element.20.weight_ref, f32[1,2048]{1,0:T(1,128)} %unstack.25.center_ref, f32[1,2048]{1,0:T(1,128)} %unstack.27.offset_ref, ...), custom_call_target="tpu_custom_call" | custom-call | flops 8999999488 | bytes 6291456 | tf_op jit(solution)/shard_map/panel/pallas_call | solution.py:347
  126.1 1.8 collective-permute-start.2
  127.9 12.7 %panel.7 = (bf16[4,96,1024]{2,1,0:T(8,128)(2,1)}, f32[4,96,1024]{2,1,0:T(8,128)}) custom-call(s32[1]{0:T(128)} %bitcast.14.side_ref, f32[8192,128]{1,0:T(8,128)} %get-tuple-element.19.pole_ref, f32[8192,128]{1,0:T(8,128)} %get-tuple-element.20.weight_ref, f32[1,2048]{1,0:T(1,128)} %unstack.25.center_ref, f32[1,2048]{1,0:T(1,128)} %unstack.27.offset_ref, ...), custom_call_target="tpu_custom_call" | custom-call | flops 8999999488 | bytes 6291456 | tf_op jit(solution)/shard_map/panel/pallas_call | solution.py:347
  140.5 0.3 collective-permute-start.3
  141.4 0.7 dynamic-slice_bitcast_fusion
  142.1 1.3 dynamic_slice.58
  143.4 1.3 dynamic_slice.59
  144.9 1.0 copy.19
  145.9 1.0 copy.20
  147.0 1.4 convert_reduce_fusion.1
  148.3 0.6 multiply_convert_fusion
  148.9 0.6 maximum_add_fusion.radius_ref
  149.5 1.5 convert_add_fusion.3
  151.0 0.9 fusion.10
  151.9 1.3 collective-permute-start.4
  153.2 2.5 collective-permute-start.5
  155.7 1.1 collective-permute-start.6
  156.8 1.6 convert_add_fusion.2
  158.4 0.9 fusion.13
  159.4 0.9 collective-permute-start.7
  160.3 1.5 convert_add_fusion.1
  161.8 0.9 fusion.16
  162.7 6.4 %collective-permute-done.3 = bf16[4,96,1024]{2,1,0:T(8,128)(2,1)} collective-permute-done((bf16[4,96,1024]{2,1,0:T(8,128)(2,1)}, bf16[4,96,1024]{2,1,0:T(8,128)(2,1)}, u32[]{:S(2)}, u32[]{:S(2)}) %collective-permute-start.3) | collective-permute-done | bytes 786464 | tf_op jit(solution)/shard_map/ppermute | solution.py:392
  169.1 1.9 collective-permute-start.8
  171.0 1.4 convert_add_fusion
  172.4 0.9 fusion.19
  173.2 0.7 broadcast_in_dim.4.geometry_ref
  173.9 24.5 %coefficients.1.coeff_ref = bf16[16,16,128,256]{3,2,1,0:T(8,128)(2,1)} custom-call(f32[4,16,128]{2,1,0:T(8,128)} %broadcast_in_dim.4.geometry_ref, f32[16,32,128]{2,1,0:T(8,128)} %bitcast.122, f32[16,32,128]{2,1,0:T(8,128)} %bitcast.123, bf16[96,1024]{1,0:T(8,128)(2,1)} %get-tuple-element.63.refs_0_, bf16[96,1024]{1,0:T(8,128)(2,1)} %get-tuple-element.62.refs_1_, ...), custom_call_target="tpu_custom_call" | custom-call | flops 17999998976 | bytes 16777216 | tf_op jit(solution)/shard_map/coefficients/pallas_call | solution.py:210
  198.4 20.8 %update.3.offset_ref = f32[16,1,128]{2,1,0:T(1,128)} custom-call(s32[2,16]{1,0:T(2,128)} %get-tuple-element.67.near_ref, f32[16]{0:T(128)} %copy-done.12, f32[16]{0:T(128)} %maximum_add_fusion.radius_ref, s32[1]{0:T(128)} %bitcast.7.first_ref, f32[512,128]{1,0:T(8,128)} %bitcast.113, f32[512,128]{1,0:T(8,128)} %bitcast.119, f32[16,1,128]{2,1,0:T(1,128)} %bitcast.130, ...), custom_call_target="tpu_custom_call" | custom-call | flops 17999998976 | bytes 16777216 | tf_op jit(solution)/shard_map/update/pallas_call | solution.py:230
  219.2 21.0 %update.4.offset_ref = f32[16,1,128]{2,1,0:T(1,128)} custom-call(s32[2,16]{1,0:T(2,128)} %get-tuple-element.67.near_ref, f32[16]{0:T(128)} %copy-done.12, f32[16]{0:T(128)} %maximum_add_fusion.radius_ref, s32[1]{0:T(128)} %bitcast.7.first_ref, f32[512,128]{1,0:T(8,128)} %bitcast.114, f32[512,128]{1,0:T(8,128)} %bitcast.120, f32[16,1,128]{2,1,0:T(1,128)} %bitcast.131, ...), custom_call_target="tpu_custom_call" | custom-call | flops 17999998976 | bytes 16777216 | tf_op jit(solution)/shard_map/update/pallas_call | solution.py:230
  240.2 20.8 %update.5 = f32[16,1,128]{2,1,0:T(1,128)} custom-call(s32[2,16]{1,0:T(2,128)} %get-tuple-element.67.near_ref, f32[16]{0:T(128)} %copy-done.12, f32[16]{0:T(128)} %maximum_add_fusion.radius_ref, s32[1]{0:T(128)} %bitcast.7.first_ref, f32[512,128]{1,0:T(8,128)} %bitcast.115, f32[512,128]{1,0:T(8,128)} %bitcast.121, f32[16,1,128]{2,1,0:T(1,128)} %bitcast.132, ...), custom_call_target="tpu_custom_call" | custom-call | flops 17999998976 | bytes 16777216 | tf_op jit(solution)/shard_map/update/pallas_call | solution.py:230
  261.1 8.8 %gather.5 = f32[8,16,128]{2,1,0:T(8,128)} custom-call(f32[16,128]{1,0:T(8,128)} %bitcast.129), custom_call_target="tpu_custom_call" | custom-call | tf_op jit(solution)/shard_map/gather/pallas_call | solution.py:76
  269.9 1.9 collective-permute-start.9
  272.0 0.9 collective-permute-start.11
  272.9 1.4 fusion.7
  274.3 2.8 collective-permute-start.12
  277.1 0.6 collective-permute-start.13
  277.7 5.5 %collective-permute-done.9 = bf16[96,1024]{1,0:T(8,128)(2,1)S(1)} collective-permute-done((bf16[96,1024]{1,0:T(8,128)(2,1)}, bf16[96,1024]{1,0:T(8,128)(2,1)S(1)}, u32[]{:S(2)}, u32[]{:S(2)}) %collective-permute-start.9) | collective-permute-done | bytes 196640 | tf_op jit(solution)/shard_map/ppermute | solution.py:399
  283.2 2.3 collective-permute-start.14
  285.5 1.3 fusion.5
  286.9 3.8 %collective-permute-start.15 = (bf16[96,1024]{1,0:T(8,128)(2,1)S(1)}, bf16[96,1024]{1,0:T(8,128)(2,1)S(1)}, u32[]{:S(2)}, u32[]{:S(2)}) collective-permute-start(bf16[96,1024]{1,0:T(8,128)(2,1)S(1)} %copy-done.9), channel_id=1, source_target_pairs={{0,24},{4,28},{8,0},{12,4},{16,8},{20,12},{24,16},{28,20},{1,25},{... | collective-permute-start | bytes 589832 | tf_op jit(solution)/shard_map/ppermute | solution.py:399
  290.7 8.3 %collective-permute-done.11 = bf16[96,1024]{1,0:T(8,128)(2,1)S(1)} collective-permute-done((bf16[96,1024]{1,0:T(8,128)(2,1)}, bf16[96,1024]{1,0:T(8,128)(2,1)S(1)}, u32[]{:S(2)}, u32[]{:S(2)}) %collective-permute-start.11) | collective-permute-done | bytes 196640 | tf_op jit(solution)/shard_map/ppermute | solution.py:399
  299.2 7.6 %collective-permute-done.14 = bf16[96,1024]{1,0:T(8,128)(2,1)S(1)} collective-permute-done((bf16[96,1024]{1,0:T(8,128)(2,1)S(1)}, bf16[96,1024]{1,0:T(8,128)(2,1)S(1)}, u32[]{:S(2)}, u32[]{:S(2)}) %collective-permute-start.14) | collective-permute-done | bytes 196640 | tf_op jit(solution)/shard_map/ppermute | solution.py:399
  307.1 2.4 copy.22
  309.5 0.6 copy.26
  (53 shorter events, 1.9 us)
Async XLA Ops:
  0.6 59.0 %copy-start.11 = (s32[2,4096]{1,0:T(2,128)S(1)}, s32[2,4096]{1,0:T(2,128)}, u32[]{:S(2)}) copy-start(s32[2,4096]{1,0:T(2,128)} %param.12) | copy-start | bytes 98308
  98.7 50.9 %collective-permute-start = (bf16[4,96,1024]{2,1,0:T(8,128)(2,1)}, bf16[4,96,1024]{2,1,0:T(8,128)(2,1)}, u32[]{:S(2)}, u32[]{:S(2)}) collective-permute-start(bf16[4,96,1024]{2,1,0:T(8,128)(2,1)} %get-tuple-element.25), channel_id=1, source_target_pairs={{0,4},{4,0},{8,12},{12,8},{16,20},{20,16},{24,28},{28,24},{1,5},{5... | collective-permute-start | bytes 2359304 | tf_op jit(solution)/shard_map/ppermute | solution.py:392
  113.1 42.6 %collective-permute-start.1 = (bf16[4,96,1024]{2,1,0:T(8,128)(2,1)}, bf16[4,96,1024]{2,1,0:T(8,128)(2,1)}, u32[]{:S(2)}, u32[]{:S(2)}) collective-permute-start(bf16[4,96,1024]{2,1,0:T(8,128)(2,1)} %get-tuple-element.27), channel_id=1, source_target_pairs={{0,4},{4,0},{8,12},{12,8},{16,20},{20,16},{24,28},{28,24},{1,5},{5... | collective-permute-start | bytes 2359304 | tf_op jit(solution)/shard_map/ppermute | solution.py:392
  126.0 14.8 %copy-start = (f32[8,64,128]{2,1,0:T(8,128)S(1)}, f32[8,64,128]{2,1,0:T(8,128)}, u32[]{:S(2)}) copy-start(f32[8,64,128]{2,1,0:T(8,128)} %get-tuple-element.17) | copy-start | bytes 786436
  126.0 15.1 %copy-start.3 = (f32[8,64,128]{2,1,0:T(8,128)S(1)}, f32[8,64,128]{2,1,0:T(8,128)}, u32[]{:S(2)}) copy-start(f32[8,64,128]{2,1,0:T(8,128)} %get-tuple-element.18) | copy-start | bytes 786436
  126.1 33.3 %collective-permute-start.2 = (bf16[4,96,1024]{2,1,0:T(8,128)(2,1)}, bf16[4,96,1024]{2,1,0:T(8,128)(2,1)}, u32[]{:S(2)}, u32[]{:S(2)}) collective-permute-start(bf16[4,96,1024]{2,1,0:T(8,128)(2,1)} %get-tuple-element.29), channel_id=1, source_target_pairs={{0,4},{4,0},{8,12},{12,8},{16,20},{20,16},{24,28},{28,24},{1,5},{5... | collective-permute-start | bytes 2359304 | tf_op jit(solution)/shard_map/ppermute | solution.py:392
  140.5 28.6 %collective-permute-start.3 = (bf16[4,96,1024]{2,1,0:T(8,128)(2,1)}, bf16[4,96,1024]{2,1,0:T(8,128)(2,1)}, u32[]{:S(2)}, u32[]{:S(2)}) collective-permute-start(bf16[4,96,1024]{2,1,0:T(8,128)(2,1)} %get-tuple-element.31), channel_id=1, source_target_pairs={{0,4},{4,0},{8,12},{12,8},{16,20},{20,16},{24,28},{28,24},{1,5},{5... | collective-permute-start | bytes 2359304 | tf_op jit(solution)/shard_map/ppermute | solution.py:392
  144.9 6.1 %copy-start.12 = (f32[16]{0:T(128)}, f32[16]{0:T(128)S(1)}, u32[]{:S(2)}) copy-start(f32[16]{0:T(128)S(1)} %get-tuple-element.49.middle_ref) | copy-start | bytes 196
  145.9 3.6 %copy-start.7 = (f32[4,96,1024]{2,1,0:T(8,128)S(1)}, f32[4,96,1024]{2,1,0:T(8,128)}, u32[]{:S(2)}) copy-start(f32[4,96,1024]{2,1,0:T(8,128)} %get-tuple-element.24) | copy-start | bytes 4718596
  149.5 7.3 %copy-start.6 = (f32[4,96,1024]{2,1,0:T(8,128)S(1)}, f32[4,96,1024]{2,1,0:T(8,128)}, u32[]{:S(2)}) copy-start(f32[4,96,1024]{2,1,0:T(8,128)} %get-tuple-element.26) | copy-start | bytes 4718596
  151.0 5.8 %copy-start.2 = (f32[4,96,1024]{2,1,0:T(8,128)}, f32[4,96,1024]{2,1,0:T(8,128)S(1)}, u32[]{:S(2)}) copy-start(f32[4,96,1024]{2,1,0:T(8,128)S(1)} %convert_add_fusion.3) | copy-start | bytes 4718596
  151.9 118.0 %collective-permute-start.4 = (bf16[96,1024]{1,0:T(8,128)(2,1)}, bf16[96,1024]{1,0:T(8,128)(2,1)}, u32[]{:S(2)}, u32[]{:S(2)}) collective-permute-start(bf16[96,1024]{1,0:T(8,128)(2,1)} %get-tuple-element.63.refs_0_), channel_id=1, source_target_pairs={{0,8},{4,12},{8,16},{12,20},{16,24},{20,28},{24,0},{28,4},{1,9},{5... | collective-permute-start | bytes 589832 | tf_op jit(solution)/shard_map/ppermute | solution.py:399
  153.2 118.6 %collective-permute-start.5 = (bf16[96,1024]{1,0:T(8,128)(2,1)}, bf16[96,1024]{1,0:T(8,128)(2,1)}, u32[]{:S(2)}, u32[]{:S(2)}) collective-permute-start(bf16[96,1024]{1,0:T(8,128)(2,1)} %get-tuple-element.62.refs_1_), channel_id=1, source_target_pairs={{0,16},{4,20},{8,24},{12,28},{16,0},{20,4},{24,8},{28,12},{1,17},{... | collective-permute-start | bytes 589832 | tf_op jit(solution)/shard_map/ppermute | solution.py:399
  155.7 116.3 %collective-permute-start.6 = (bf16[96,1024]{1,0:T(8,128)(2,1)}, bf16[96,1024]{1,0:T(8,128)(2,1)}, u32[]{:S(2)}, u32[]{:S(2)}) collective-permute-start(bf16[96,1024]{1,0:T(8,128)(2,1)} %get-tuple-element.61.refs_2_), channel_id=1, source_target_pairs={{0,24},{4,28},{8,0},{12,4},{16,8},{20,12},{24,16},{28,20},{1,25},{... | collective-permute-start | bytes 589832 | tf_op jit(solution)/shard_map/ppermute | solution.py:399
  156.8 3.5 %copy-start.5 = (f32[4,96,1024]{2,1,0:T(8,128)S(1)}, f32[4,96,1024]{2,1,0:T(8,128)}, u32[]{:S(2)}) copy-start(f32[4,96,1024]{2,1,0:T(8,128)} %get-tuple-element.28) | copy-start | bytes 4718596
  158.4 3.4 %copy-start.1 = (f32[4,96,1024]{2,1,0:T(8,128)}, f32[4,96,1024]{2,1,0:T(8,128)S(1)}, u32[]{:S(2)}) copy-start(f32[4,96,1024]{2,1,0:T(8,128)S(1)} %convert_add_fusion.2) | copy-start | bytes 4718596
  159.4 115.0 %collective-permute-start.7 = (bf16[96,1024]{1,0:T(8,128)(2,1)}, bf16[96,1024]{1,0:T(8,128)(2,1)}, u32[]{:S(2)}, u32[]{:S(2)}) collective-permute-start(bf16[96,1024]{1,0:T(8,128)(2,1)} %get-tuple-element.60.refs_3_), channel_id=1, source_target_pairs={{0,8},{4,12},{8,16},{12,20},{16,24},{20,28},{24,0},{28,4},{1,9},{5... | collective-permute-start | bytes 589832 | tf_op jit(solution)/shard_map/ppermute | solution.py:399
  160.3 10.7 %copy-start.4 = (f32[4,96,1024]{2,1,0:T(8,128)S(1)}, f32[4,96,1024]{2,1,0:T(8,128)}, u32[]{:S(2)}) copy-start(f32[4,96,1024]{2,1,0:T(8,128)} %get-tuple-element.30) | copy-start | bytes 4718596
  169.1 108.0 %collective-permute-start.8 = (bf16[96,1024]{1,0:T(8,128)(2,1)}, bf16[96,1024]{1,0:T(8,128)(2,1)}, u32[]{:S(2)}, u32[]{:S(2)}) collective-permute-start(bf16[96,1024]{1,0:T(8,128)(2,1)} %get-tuple-element.59.refs_4_), channel_id=1, source_target_pairs={{0,16},{4,20},{8,24},{12,28},{16,0},{20,4},{24,8},{28,12},{1,17},{... | collective-permute-start | bytes 589832 | tf_op jit(solution)/shard_map/ppermute | solution.py:399
  240.2 43.0 %copy-start.10 = (bf16[96,1024]{1,0:T(8,128)(2,1)S(1)}, bf16[96,1024]{1,0:T(8,128)(2,1)}, u32[]{:S(2)}) copy-start(bf16[96,1024]{1,0:T(8,128)(2,1)} %get-tuple-element.53.refs_1_) | copy-start | bytes 589828
  261.1 25.8 %copy-start.9 = (bf16[96,1024]{1,0:T(8,128)(2,1)S(1)}, bf16[96,1024]{1,0:T(8,128)(2,1)}, u32[]{:S(2)}) copy-start(bf16[96,1024]{1,0:T(8,128)(2,1)} %get-tuple-element.52.refs_2_) | copy-start | bytes 589828
  269.9 13.3 %collective-permute-start.9 = (bf16[96,1024]{1,0:T(8,128)(2,1)}, bf16[96,1024]{1,0:T(8,128)(2,1)S(1)}, u32[]{:S(2)}, u32[]{:S(2)}) collective-permute-start(bf16[96,1024]{1,0:T(8,128)(2,1)} %get-tuple-element.58.refs_5_), channel_id=1, source_target_pairs={{0,24},{4,28},{8,0},{12,4},{16,8},{20,12},{24,16},{28,20},{1,25},{... | collective-permute-start | bytes 589832 | tf_op jit(solution)/shard_map/ppermute | solution.py:399
  271.8 15.1 %collective-permute-start.10 = (bf16[96,1024]{1,0:T(8,128)(2,1)}, bf16[96,1024]{1,0:T(8,128)(2,1)S(1)}, u32[]{:S(2)}, u32[]{:S(2)}) collective-permute-start(bf16[96,1024]{1,0:T(8,128)(2,1)} %get-tuple-element.57.refs_0_), channel_id=1, source_target_pairs={{0,8},{4,12},{8,16},{12,20},{16,24},{20,28},{24,0},{28,4},{1,9},{5... | collective-permute-start | bytes 589832 | tf_op jit(solution)/shard_map/ppermute | solution.py:399
  272.0 27.0 %collective-permute-start.11 = (bf16[96,1024]{1,0:T(8,128)(2,1)}, bf16[96,1024]{1,0:T(8,128)(2,1)S(1)}, u32[]{:S(2)}, u32[]{:S(2)}) collective-permute-start(bf16[96,1024]{1,0:T(8,128)(2,1)} %get-tuple-element.56.refs_1_), channel_id=1, source_target_pairs={{0,16},{4,20},{8,24},{12,28},{16,0},{20,4},{24,8},{28,12},{1,17},{... | collective-permute-start | bytes 589832 | tf_op jit(solution)/shard_map/ppermute | solution.py:399
  274.3 24.7 %collective-permute-start.12 = (bf16[96,1024]{1,0:T(8,128)(2,1)}, bf16[96,1024]{1,0:T(8,128)(2,1)S(1)}, u32[]{:S(2)}, u32[]{:S(2)}) collective-permute-start(bf16[96,1024]{1,0:T(8,128)(2,1)} %get-tuple-element.55.refs_2_), channel_id=1, source_target_pairs={{0,24},{4,28},{8,0},{12,4},{16,8},{20,12},{24,16},{28,20},{1,25},{... | collective-permute-start | bytes 589832 | tf_op jit(solution)/shard_map/ppermute | solution.py:399
  277.1 22.1 %collective-permute-start.13 = (bf16[96,1024]{1,0:T(8,128)(2,1)}, bf16[96,1024]{1,0:T(8,128)(2,1)S(1)}, u32[]{:S(2)}, u32[]{:S(2)}) collective-permute-start(bf16[96,1024]{1,0:T(8,128)(2,1)} %get-tuple-element.54.refs_0_), channel_id=1, source_target_pairs={{0,8},{4,12},{8,16},{12,20},{16,24},{20,28},{24,0},{28,4},{1,9},{5... | collective-permute-start | bytes 589832 | tf_op jit(solution)/shard_map/ppermute | solution.py:399
  283.2 23.6 %collective-permute-start.14 = (bf16[96,1024]{1,0:T(8,128)(2,1)S(1)}, bf16[96,1024]{1,0:T(8,128)(2,1)S(1)}, u32[]{:S(2)}, u32[]{:S(2)}) collective-permute-start(bf16[96,1024]{1,0:T(8,128)(2,1)S(1)} %copy-done.10), channel_id=1, source_target_pairs={{0,16},{4,20},{8,24},{12,28},{16,0},{20,4},{24,8},{28,12},{1,17},{... | collective-permute-start | bytes 589832 | tf_op jit(solution)/shard_map/ppermute | solution.py:399
  286.9 20.0 %collective-permute-start.15 = (bf16[96,1024]{1,0:T(8,128)(2,1)S(1)}, bf16[96,1024]{1,0:T(8,128)(2,1)S(1)}, u32[]{:S(2)}, u32[]{:S(2)}) collective-permute-start(bf16[96,1024]{1,0:T(8,128)(2,1)S(1)} %copy-done.9), channel_id=1, source_target_pairs={{0,24},{4,28},{8,0},{12,4},{16,8},{20,12},{24,16},{28,20},{1,25},{... | collective-permute-start | bytes 589832 | tf_op jit(solution)/shard_map/ppermute | solution.py:399
  307.1 2.4 copy-start.8

commit v2 on v1

--- a/solution.py
+++ b/solution.py
@@ -1,3 +1,4 @@
+import functools
 import itertools
 import jax
 import jax.numpy as jnp
@@ -16,7 +17,6 @@
 PIECES = 3
 WIDTH = 256
 DEPTH = 1024
-PARTS = 2
 FLOPS_PER_US = 1_000_000_000
 
 
@@ -84,22 +84,20 @@
     )(*[v for v, _ in items])
 
 
-def coefficients_kernel(geometry_ref, block_poles_ref, block_weights_ref, *refs):
-    coeff_ref, top_ref, bottom_ref = refs[-3:]
-    q = pl.program_id(1)
+def coefficients(geometry, poles, weights, q, coeff_ref, at, top_ref, bottom_ref):
     blank = jnp.zeros((8, LANES), jnp.float32)
     for k in range(BLOCK, TERMS):
         top_ref[8 * k : 8 * k + 8, :] = blank
         bottom_ref[8 * k : 8 * k + 8, :] = blank
-    middle, radius, first, last = (geometry_ref[i] for i in range(4))
+    middle, radius, first, last = geometry
     inverse_radius = 1.0 / radius
     block = (q * LANES + lax.broadcasted_iota(jnp.int32, (8, LANES), 1)).astype(jnp.float32)
     far = jnp.logical_or(block < first, block >= last)
     scale = jnp.where(far, radius, 0.0)
     top, bottom = [], [jnp.ones((8, LANES), jnp.float32)]
     for j in range(BLOCK):
-        weight = block_weights_ref[0, j : j + 1, :]
-        ratio = scale / (block_poles_ref[0, j : j + 1, :] - middle)
+        weight = weights[j : j + 1, :]
+        ratio = scale / (poles[j : j + 1, :] - middle)
         value = (weight * weight) * ratio * inverse_radius
         new_top, new_bottom = [], []
         for k in range(j + 1):
@@ -121,16 +119,16 @@
     for k in range(BLOCK + 1):
         bottom_ref[8 * k : 8 * k + 8, :] = bottom[k]
     for member in range(coeff_ref.shape[0]):
-        for ref, at in ((top_ref, 0), (bottom_ref, LANES)):
+        for ref, lane in ((top_ref, 0), (bottom_ref, LANES)):
             high, low = pieces(ref[pl.ds(member, TERMS, stride=8), :])
             rows = jnp.concatenate([high, low, high, blank], axis=0)
-            coeff_ref[member, 0, :, at : at + LANES] = rows.astype(jnp.bfloat16)
-
-
-def update_kernel(near_ref, middle_ref, radius_ref, first_ref, poles_ref, weights_ref, center_ref, offset_ref, coeff_ref, *refs):
-    out_ref = refs[-1]
-    tile = pl.program_id(0)
-    chunks = coeff_ref.shape[1]
+            coeff_ref[member, at, :, lane : lane + LANES] = rows.astype(jnp.bfloat16)
+
+
+def update_kernel(count, base, near_ref, middle_ref, radius_ref, first_ref, poles_ref, weights_ref, center_ref, offset_ref, *refs):
+    coeff_refs, out_ref = refs[:count], refs[-1]
+    step = pl.program_id(0)
+    tile = base + step
     order = lax.broadcasted_iota(jnp.int32, (TERMS, LANES), 0)
     blank = jnp.zeros((8, LANES), jnp.float32)
 
@@ -146,15 +144,15 @@
     slope_rows = to_rows(order.astype(jnp.float32) * power(ratio, jnp.maximum(order - 1, 0)))
     rows = jnp.concatenate([value_rows, slope_rows], axis=0)
     inverse_sum = square_sum = None
-    for q in range(chunks):
-        got = jnp.dot(rows, coeff_ref[0, q], preferred_element_type=jnp.float32)
+    for ref, q in [(ref, q) for ref in coeff_refs for q in range(ref.shape[1])]:
+        got = jnp.dot(rows, ref[0, q], preferred_element_type=jnp.float32)
         top, bottom = got[:LANES, :LANES], got[:LANES, LANES:]
         top_slope, bottom_slope = got[LANES:, :LANES], got[LANES:, LANES:]
         inverse = 1.0 / bottom
         quotient = top * inverse
         slope = (top_slope - quotient * bottom_slope) * inverse
-        inverse_sum = quotient if q == 0 else inverse_sum + quotient
-        square_sum = slope if q == 0 else square_sum + slope
+        inverse_sum = quotient if inverse_sum is None else inverse_sum + quotient
+        square_sum = slope if square_sum is None else square_sum + slope
     square_sum = square_sum / radius
     place_rows = jnp.broadcast_to(place, (LANES, LANES)).T
     inverse_parts, square_parts = [], []
@@ -189,7 +187,7 @@
     out_ref[0] = offset - jnp.minimum(jnp.maximum(change, -limit), limit)
 
 
-def find_roots(poles, weights, centers, offsets, my_first, after):
+def prepare(poles, weights, centers):
     flat = lambda values: values.reshape(-1, LANES)
     tiles = centers.shape[0] // LANES
     chunks = poles.shape[0] // (BLOCK * LANES)
@@ -201,42 +199,33 @@
     unit = PAIR * LANES
     near = jnp.stack([below // unit, (inside + unit - 1) // unit])
     limits = (near * (unit // BLOCK)).astype(jnp.float32)
-    octet = min(tiles, 8)
     geometry = jnp.stack([middle, radius, limits[0], limits[1]])
     geometry = jnp.pad(geometry, ((0, 0), (0, -tiles % 8)), mode="edge")
     geometry = jnp.broadcast_to(geometry[:, :, None], geometry.shape + (LANES,))
     blocked = lambda values: values.reshape(chunks, LANES, BLOCK).transpose(0, 2, 1)
+    return near, middle, radius, geometry, blocked(poles), blocked(weights)
+
+
+def update(prepared, poles, weights, centers, now, my_first, base, coeffs, after):
+    near, middle, radius = prepared[:3]
+    flat = lambda values: values.reshape(-1, LANES)
     smem, anywhere = pl.BlockSpec(memory_space=pltpu.SMEM), pl.BlockSpec(memory_space=pl.ANY)
-    coeff = pl.pallas_call(
-        coefficients_kernel,
-        grid=(geometry.shape[1] // 8, chunks),
-        out_shape=jax.ShapeDtypeStruct((tiles, chunks, LANES, 2 * LANES), jnp.bfloat16),
-        in_specs=[
-            pl.BlockSpec((4, 8, LANES), lambda o, q: (0, o, 0)),
-            pl.BlockSpec((1, BLOCK, LANES), lambda o, q: (q, 0, 0)),
-            pl.BlockSpec((1, BLOCK, LANES), lambda o, q: (q, 0, 0)),
-        ] + [anywhere] * len(after[0]),
-        out_specs=pl.BlockSpec((octet, 1, LANES, 2 * LANES), lambda o, q: (o, q, 0, 0)),
-        scratch_shapes=[pltpu.VMEM((8 * TERMS, LANES), jnp.float32)] * 2,
-        cost_estimate=pl.CostEstimate(flops=FLOPS_PER_US * 18, bytes_accessed=tiles * chunks * LANES * LANES * 4, transcendentals=0),
-        name="coefficients",
-    )(geometry, blocked(poles), blocked(weights), *after[0])
     whole = pl.BlockSpec((poles.shape[0] // LANES, LANES), lambda t: (0, 0))
+    tiles = coeffs[0].shape[0]
     one = pl.BlockSpec((1, 1, LANES), lambda t: (t, 0, 0))
-    spread = lambda values: values.reshape(tiles, 1, LANES)
-    now = spread(offsets)
-    first = (my_first // LANES).reshape(1)
-    for step in range(ITERS):
-        now = pl.pallas_call(
-            update_kernel,
-            grid=(tiles,),
-            out_shape=jax.ShapeDtypeStruct((tiles, 1, LANES), jnp.float32),
-            in_specs=[smem] * 4 + [whole] * 2 + [one] * 2 + [pl.BlockSpec((1, chunks, LANES, 2 * LANES), lambda t: (t, 0, 0, 0))] + [anywhere] * len(after[step + 1]),
-            out_specs=one,
-            cost_estimate=pl.CostEstimate(flops=FLOPS_PER_US * 18, bytes_accessed=tiles * chunks * LANES * LANES * 4, transcendentals=0),
-            name="update",
-        )(near, middle, radius, first, flat(poles), flat(weights), spread(centers), now, coeff, *after[step + 1])
-    return now.reshape(-1)
+    return pl.pallas_call(
+        functools.partial(update_kernel, len(coeffs), base),
+        grid=(tiles,),
+        out_shape=jax.ShapeDtypeStruct((tiles, 1, LANES), jnp.float32),
+        in_specs=[smem] * 4
+        + [whole] * 2
+        + [pl.BlockSpec((1, 1, LANES), lambda t: (base + t, 0, 0)), one]
+        + [pl.BlockSpec((1,) + c.shape[1:], lambda t: (t, 0, 0, 0)) for c in coeffs]
+        + [anywhere] * len(after),
+        out_specs=one,
+        cost_estimate=pl.CostEstimate(flops=FLOPS_PER_US * 10, bytes_accessed=tiles * LANES * LANES * 64, transcendentals=0),
+        name="update",
+    )(near, middle, radius, (my_first // LANES).reshape(1), flat(poles), flat(weights), centers.reshape(-1, 1, LANES), now, *coeffs, *after)
 
 
 def lookup_kernel(index_ref, *refs):
@@ -317,7 +306,7 @@
     out_ref[...] = jnp.concatenate([spread(center), spread(offset), spread(norm), blank], axis=0)
 
 
-def panel_kernel(side_ref, pole_ref, weight_ref, center_ref, offset_ref, norm_ref, eigen_ref, send_ref, keep_ref, total_ref):
+def panel_kernel(start, chunks, side_ref, pole_ref, weight_ref, center_ref, offset_ref, norm_ref, eigen_ref, geometry_ref, block_poles_ref, block_weights_ref, send_ref, keep_ref, coeff_ref, total_ref, *refs):
     depth = eigen_ref.shape[2]
     center, offset, norm = center_ref[...], offset_ref[...], norm_ref[...]
     total = None
@@ -330,6 +319,11 @@
             columns.append((weight_ref[rows, :] * (1.0 / distance) * norm[:, lanes]).astype(jnp.bfloat16))
         part = jnp.dot(eigen_ref[0, :, rows], jnp.concatenate(columns, axis=1), preferred_element_type=jnp.float32)
         total = part if total is None else total + part
+    per = coeff_ref.shape[1]
+    for u in range(per):
+        q = lax.rem(start + pl.program_id(0) * per + u, chunks)
+        geometry = [geometry_ref[i] for i in range(4)]
+        coefficients(geometry, block_poles_ref[u], block_weights_ref[u], q, coeff_ref, u, *refs[2 * u : 2 * u + 2])
     total_ref[...] = total
     side = side_ref[0]
     size = send_ref.shape[1]
@@ -338,23 +332,61 @@
         keep_ref[z] = total_ref[pl.ds(pl.multiple_of((2 * z + side) * size, 8), size), :]
 
 
-def panel_part(side, pole, weight, panel, eigen, half, first, width, rows):
+def panel_half(side, pole, weight, panel, eigen, half, rows, prepared, tiles):
     height, depth = eigen.shape[1], eigen.shape[2]
+    width = panel[0].shape[0]
+    steps = width // WIDTH
+    geometry, block_poles, block_weights = prepared[3:]
+    chunks = block_poles.shape[0]
+    octets = geometry.shape[1] // 8
+    per = octets * chunks // (eigen.shape[0] * steps)
+    start = half * steps * per
+    octet, members = start // chunks, min(tiles, 8)
     shape = (rows // 2, height // rows, width)
-    row = pl.BlockSpec((1, WIDTH), lambda i: (0, first // WIDTH + i))
+    row = pl.BlockSpec((1, WIDTH), lambda i: (0, i))
     wide = pl.BlockSpec((depth, LANES), lambda i: (half, 0))
     out = pl.BlockSpec(shape[:2] + (WIDTH,), lambda i: (0, 0, i))
+    blocks = pl.BlockSpec((per, BLOCK, LANES), lambda i: (start % chunks // per + i, 0, 0))
     return pl.pallas_call(
-        panel_kernel,
-        grid=(width // WIDTH,),
-        out_shape=[jax.ShapeDtypeStruct(shape, jnp.bfloat16), jax.ShapeDtypeStruct(shape, jnp.float32)],
-        in_specs=[pl.BlockSpec(memory_space=pltpu.SMEM), wide, wide, row, row, row, pl.BlockSpec((1, height, depth), lambda i: (half, 0, 0))],
-        out_specs=[out, out],
-        scratch_shapes=[pltpu.VMEM((height, WIDTH), jnp.float32)],
-        cost_estimate=pl.CostEstimate(flops=FLOPS_PER_US * 9, bytes_accessed=height * depth * 2, transcendentals=0),
-        compiler_params=pltpu.CompilerParams(vmem_limit_bytes=56 * 1024 * 1024),
+        functools.partial(panel_kernel, start, chunks),
+        grid=(steps,),
+        out_shape=[
+            jax.ShapeDtypeStruct(shape, jnp.bfloat16),
+            jax.ShapeDtypeStruct(shape, jnp.float32),
+            jax.ShapeDtypeStruct((members, steps * per, LANES, 2 * LANES), jnp.bfloat16),
+        ],
+        in_specs=[pl.BlockSpec(memory_space=pltpu.SMEM), wide, wide, row, row, row, pl.BlockSpec((1, height, depth), lambda i: (half, 0, 0))]
+        + [pl.BlockSpec((4, 8, LANES), lambda i: (0, octet, 0)), blocks, blocks],
+        out_specs=[out, out, pl.BlockSpec((members, per, LANES, 2 * LANES), lambda i: (0, i, 0, 0))],
+        scratch_shapes=[pltpu.VMEM((height, WIDTH), jnp.float32)] + [pltpu.VMEM((8 * TERMS, LANES), jnp.float32)] * (2 * per),
+        cost_estimate=pl.CostEstimate(flops=FLOPS_PER_US * 22, bytes_accessed=height * depth * 2, transcendentals=0),
+        compiler_params=pltpu.CompilerParams(vmem_limit_bytes=60 * 1024 * 1024),
         name="panel",
-    )(side, pole, weight, *[p[None, :] for p in panel], eigen)
+    )(side, pole, weight, *[p[None, :] for p in panel], eigen, geometry, block_poles, block_weights)
+
+
+def merge_kernel(deep_ref, keep_ref, met_ref, own_ref, *block_refs):
+    count = keep_ref.shape[0]
+    deep = deep_ref[0]
+    for shift, ref in enumerate((own_ref,) + block_refs):
+        at = lax.rem(deep + shift, count)
+        ref[...] = (keep_ref[at] + met_ref[at].astype(jnp.float32)).astype(ref.dtype)
+
+
+def merge(deep, keep, met):
+    count, height, width = keep.shape
+    size = WIDTH * 2
+    whole = pl.BlockSpec((count, height, size), lambda i: (0, 0, i))
+    block = pl.BlockSpec((height, size), lambda i: (0, i))
+    return pl.pallas_call(
+        merge_kernel,
+        grid=(width // size,),
+        out_shape=[jax.ShapeDtypeStruct((height, width), jnp.bfloat16 if s else jnp.float32) for s in range(count)],
+        in_specs=[pl.BlockSpec(memory_space=pltpu.SMEM), whole, whole],
+        out_specs=[block] * count,
+        cost_estimate=pl.CostEstimate(flops=FLOPS_PER_US * 2, bytes_accessed=keep.size * 8, transcendentals=0),
+        name="merge",
+    )(deep.reshape(1), keep, met)
 
 
 def on_device(pole_values, weights, centers, offsets, chosen, column_pole, eigen_blocks):
@@ -364,56 +396,72 @@
     per_device = offsets.shape[0] // rows
     first_root = row * per_device
     my_first = col * offsets.shape[0] + first_root
-    all_poles, all_weights, all_offsets = gather_inputs(pole_values, weights, offsets)
+    all_poles, all_weights, all_offsets = gather_inputs(pole_values, weights, offsets, rows, cols)
     total = all_poles.shape[0]
 
     share = chosen.shape[0] // (rows * cols)
     mine = lax.dynamic_slice_in_dim(chosen, (row * cols + col) * share, share)
     padded = jnp.pad(mine, (0, LANES - share))
-    index = jnp.concatenate([padded, jnp.minimum(padded + 1, total - 1)])
-    found_pole, found_offset = lookup([flat(all_poles), flat(all_offsets)], index)
+    per_col = offsets.shape[0]
+    turned = lax.rem(col - padded // per_col + cols, cols) * per_col + lax.rem(padded, per_col)
+    index = jnp.concatenate([padded, jnp.minimum(padded + 1, total - 1), turned])
+    found_pole, found_offset = lookup([flat(all_poles), all_offsets], index)
     last = jnp.broadcast_to((mine == total - 1).astype(jnp.int32)[:, None], (share, LANES))
     here = pl.BlockSpec(memory_space=pltpu.VMEM)
     packed = pl.pallas_call(
         chosen_kernel, out_shape=jax.ShapeDtypeStruct((8, LANES), jnp.float32), in_specs=[here] * 6, out_specs=here, name="chosen"
-    )(flat(all_poles), flat(all_weights), last, found_pole[:LANES], found_pole[LANES:], found_offset[:LANES])
-    panel = gather([(packed, AXES)], 1)[0][:, :3, :share].transpose(1, 0, 2).reshape(3, -1)
+    )(flat(all_poles), flat(all_weights), last, found_pole[:LANES], found_pole[LANES : 2 * LANES], found_offset[2 * LANES :])
+    shared = copies(packed, AXES, rows * cols)
+    panel = shared[:, :3, :share].transpose(1, 0, 2).reshape(3, -1)
 
     pole, weight = lookup([flat(all_poles), flat(all_weights)], column_pole.reshape(-1))
     eigen = jnp.transpose(eigen_blocks, (1, 0, 2))
     side = lax.rem(row, 2).reshape(1)
     deep = row // 2
     near_pairs = [(r, r ^ 1) for r in range(rows)]
-    received, outgoing = [], []
-    width = chosen.shape[0] // PARTS
-    for half in range(column_pole.shape[0]):
-        for first in range(0, chosen.shape[0], width):
-            send, keep = panel_part(side, pole, weight, panel, eigen, half, first, width, rows)
-            met = lax.ppermute(send, "row", near_pairs)
-            both = keep + met.astype(jnp.float32)
-            blocks, arrived = [], [lax.dynamic_index_in_dim(both, deep, 0, keepdims=False)]
-            for shift in range(1, rows // 2):
-                block = lax.dynamic_index_in_dim(both, lax.rem(deep + shift, rows // 2), 0, keepdims=False)
-                blocks.append(block.astype(jnp.bfloat16))
-                pairs = [(r, (r + 2 * shift) % rows) for r in range(rows)]
-                arrived.append(lax.ppermute(blocks[-1], "row", pairs))
-            outgoing.append(blocks)
-            received.append(arrived)
-
     my_centers = lax.dynamic_slice_in_dim(centers, first_root, per_device)
     my_offsets = lax.dynamic_slice_in_dim(offsets, first_root, per_device)
-    after = [outgoing[0] + outgoing[1], outgoing[2], outgoing[3], []]
-    my_offsets = find_roots(all_poles, all_weights, my_centers, my_offsets, my_first, after)
+    prepared = prepare(all_poles, all_weights, my_centers)
+    tiles = per_device // LANES
+    received, outgoing, coeffs = [], [], []
+    for half in range(column_pole.shape[0]):
+        send, keep, coeff = panel_half(side, pole, weight, panel, eigen, half, rows, prepared, tiles)
+        coeffs.append(coeff)
+        met = lax.ppermute(send, "row", near_pairs)
+        own, *blocks = merge(deep, keep, met)
+        arrived = [own]
+        for shift, block in enumerate(blocks, 1):
+            pairs = [(r, (r + 2 * shift) % rows) for r in range(rows)]
+            arrived.append(lax.ppermute(block, "row", pairs))
+        outgoing.append(blocks)
+        received.append(arrived)
+
+    members = coeffs[0].shape[0]
+    groups = [coeffs] if members == tiles else [[c] for c in coeffs]
+    calls = [(g, step) for g in range(len(groups)) for step in range(ITERS)]
+    lates = {1: outgoing[0], len(calls) // 2: outgoing[1]}
+    latest = []
+    spread = my_offsets.reshape(tiles, 1, LANES)
+    nows = [spread[g * members : (g + 1) * members] for g in range(len(groups))]
+    for at, (g, step) in enumerate(calls):
+        nows[g] = update(prepared, all_poles, all_weights, my_centers, nows[g], my_first, g * members, groups[g], latest + lates.get(at, []))
+        latest = [nows[g]]
+    my_offsets = jnp.concatenate(nows, axis=0)
     offset_now = gather([(flat(my_offsets), ("row",))], 2)[0].reshape(-1)
     add = lambda parts: sum([p.astype(jnp.float32) for p in parts[1:]], parts[0])
-    halves = [jnp.concatenate([add(parts) for parts in received[at : at + PARTS]], axis=1) for at in range(0, len(received), PARTS)]
+    halves = [add(parts) for parts in received]
     return (offset_now, jnp.stack(halves, axis=1))
 
 
-def gather_inputs(pole_values, weights, offsets):
-    flat = lambda values: values.reshape(-1, LANES)
-    all_poles, all_weights, all_offsets = gather([(flat(pole_values), ("row",)), (flat(weights), ("row",)), (flat(offsets), ("col",))], 0)
-    return all_poles.reshape(-1), all_weights.reshape(-1), all_offsets.reshape(-1)
+def copies(value, axis, count):
+    return lax.all_to_all(jnp.broadcast_to(value[None], (count,) + value.shape), axis, 0, 0, tiled=True)
+
+
+def gather_inputs(pole_values, weights, offsets, rows, cols):
+    both = copies(jnp.stack([pole_values.reshape(-1, LANES), weights.reshape(-1, LANES)]), "row", rows)
+    own = offsets.reshape(-1, LANES)
+    turned = [own] + [lax.ppermute(own, "col", [(c, (c + shift) % cols) for c in range(cols)]) for shift in range(1, cols)]
+    return both[:, 0].reshape(-1), both[:, 1].reshape(-1), jnp.concatenate(turned, axis=0)
 
 
 def solution(mesh):

time: 314 us -> 284 us (0.904)
  Pallas kernels: 209 us -> 178 us
  other arithmetic: 13.1 us -> 7.94 us
  starting transfers between devices: 24.3 us -> 28.9 us
    pallas_call x3 -> x1, Pallas kernels: 38.8 us -> 9.1 us  [gather(): pl.pallas_call(kernel, out_shape=[jax.ShapeDtypeStruct((len(g),) + v.shap...]
    all_to_all x0 -> x2, starting transfers between devices: none -> 12.6 us  [copies(): lax.all_to_all(jnp.broadcast_to(value[None], (count,) + value.shape), axi...]
    add x10 -> x2, other arithmetic: 9.33 us -> 0.59 us  [prepare(): jnp.maximum(tile_centers[:, -1] - middle, middle - tile_centers[:, 0]) + 2.5]
    ppermute x4 -> x2, waiting for transfers between devices: 6.44 us -> 13.9 us  [on_device(): met = lax.ppermute(send, 'row', near_pairs)]
    ppermute x12 -> x9, starting transfers between devices: 20.2 us -> 14.3 us  [the longest x6 11.4 us: on_device(): arrived.append(lax.ppermute(block, 'row', pairs))]
    ppermute x12 -> x9, waiting for transfers between devices: 21.5 us -> 15.7 us  [the longest x6 15.7 us: on_device(): arrived.append(lax.ppermute(block, 'row', pairs))]
    convert_element_type x4 -> x0, local copies, waits for them, and re-layouts: 3.61 us -> none  [on_device(): blocks.append(block.astype(jnp.bfloat16))]
    pallas_call x8 -> x10, Pallas kernels: 138 us -> 136 us  [the longest x6 68.5 us: update(): pl.pallas_call(functools.partial(update_kernel, len(coeffs), base), grid=...]
  transfers between devices with their start and end apart: 16 -> 13, of which waited for: 4 -> 2; matrix products, arithmetic and copies ran while one was open for 7% -> 11% of each run, Pallas kernels for 43% -> 45%
where the time goes in v2:
time: 284 us; the launch traced here: 282 us
  Pallas kernels  178 us (63%)
  local copies, waits for them, and re-layouts  36.7 us (13%)
  waiting for transfers between devices  29.6 us (10%)
  starting transfers between devices  28.9 us (10%)
  other arithmetic  7.94 us (3%)
    pallas_call x6, Pallas kernels, update(): pl.pallas_call(functools.partial(update_kernel, len(coeffs), base), grid=...  68.5 us
    pallas_call x2, Pallas kernels, panel_half(): pl.pallas_call(functools.partial(panel_kernel, start, chunks), grid=(step...  59.3 us
    unnamed x17, local copies, waits for them, and re-layouts  18.7 us
    pallas_call x1, Pallas kernels, on_device(): pl.pallas_call(chosen_kernel, out_shape=jax.ShapeDtypeStruct((8, LANES),...  18.6 us
    ppermute x6, waiting for transfers between devices, on_device(): arrived.append(lax.ppermute(block, 'row', pairs))  15.7 us
    ppermute x2, waiting for transfers between devices, on_device(): met = lax.ppermute(send, 'row', near_pairs)  13.9 us
    pallas_call x2, Pallas kernels, lookup(): pl.pallas_call(lookup_kernel, grid=(groups // step,), out_shape=[jax.Shap...  13.8 us
    all_to_all x2, starting transfers between devices, copies(): lax.all_to_all(jnp.broadcast_to(value[None], (count,) + value.shape), axi...  12.6 us
  transfers between devices with their start and end apart: 13, of which 2 were waited for; matrix products, arithmetic and copies ran while one was open for 11% of the time, Pallas kernels for 45%

profile of v2, /device:TPU:0, one launch (start us, length us, event | category | flops | bytes accessed | tf_op | source)
XLA Modules:
  0.0 281.7 jit_solution(12171560233067129289)
XLA Ops:
  0.6 0.8 pad_maximum_fusion.2
  1.4 0.8 broadcast_in_dim.8
  2.3 7.3 %all-to-all-start = ((f32[8,2,64,128]{3,2,1,0:T(8,128)}), f32[8,2,64,128]{3,2,1,0:T(8,128)S(1)}, u32[]{:S(2)}, u32[]{:S(2)}) async-start(f32[8,2,64,128]{3,2,1,0:T(8,128)} %broadcast_in_dim.8), calls=%async_computation | async-start | bytes 1048576 | tf_op jit(solution)/shard_map/all_to_all | solution.py:457
  9.5 0.0 collective-permute-start
  9.5 1.6 collective-permute-start.1
  11.1 1.4 collective-permute-start.2
  12.5 1.4 reshape_reshape.3.index_ref
  13.9 14.5 %copy.38 = bf16[768,2,4096]{2,0,1:T(8,128)(2,1)} copy(bf16[768,2,4096]{2,1,0:T(2,128)(2,1)} %param.13) | data formatting | bytes 25165824 | tf_op args[6]
  28.5 0.8 compare_convert_fusion
  29.2 0.7 dynamic-slice_bitcast_fusion
  29.9 0.2 slice_reduce_fusion.4
  30.2 0.6 pad_add_fusion.index_ref
  30.8 0.7 pad_maximum_fusion.1.refs_1_
  31.5 0.8 fusion.6
  32.3 2.5 lookup.3
  34.8 1.5 fusion.7
  36.4 1.5 slice.70.start_ref
  37.8 0.7 broadcast_in_dim.9.last_ref
  38.5 18.6 %chosen.1 = f32[8,128]{1,0:T(8,128)} custom-call(f32[512,128]{1,0:T(8,128)} %bitcast.71, f32[512,128]{1,0:T(8,128)} %bitcast.80, s32[64,128]{1,0:T(8,128)} %broadcast_in_dim.9.last_ref, f32[128,128]{1,0:T(8,128)} %get-tuple-element.63.left_ref, f32[128,128]{1,0:T(8,128)} %get-tuple-element.62.right_ref, f32[128,128]{1,0:T(8,128)} %slice.70.start_ref), custom_call_target="tpu_custom_call" | custom-call | tf_op jit(solution)/shard_map/chosen/pallas_call | solution.py:411
  57.1 1.3 broadcast_in_dim.10
  58.4 5.3 %all-to-all-start.1 = ((f32[32,8,128]{2,1,0:T(8,128)}), f32[32,8,128]{2,1,0:T(8,128)S(1)}, u32[]{:S(2)}, u32[]{:S(2)}) async-start(f32[32,8,128]{2,1,0:T(8,128)} %broadcast_in_dim.10), calls=%async_computation.1 | async-start | bytes 262144 | tf_op jit(solution)/shard_map/all_to_all | solution.py:457
  63.7 1.9 convert_reduce_fusion.1
  65.7 1.2 reshape_reshape_squeeze.10
  66.9 1.2 reshape_reshape_squeeze.11
  68.1 11.3 %lookup.2 = (f32[8192,128]{1,0:T(8,128)}, f32[8192,128]{1,0:T(8,128)}) custom-call(s32[64,1,128]{2,1,0:T(1,128)} %reshape_reshape.3.index_ref, f32[512,128]{1,0:T(8,128)} %bitcast.73, f32[512,128]{1,0:T(8,128)} %bitcast.81), custom_call_target="tpu_custom_call" | custom-call | tf_op jit(solution)/shard_map/lookup/pallas_call | solution.py:264
  79.4 1.0 copy.32
  80.4 1.0 copy.33
  81.4 0.6 multiply_convert_fusion
  82.1 0.1 slice_reduce_fusion
  82.2 0.7 unstack.19.center_ref
  82.9 0.7 unstack.21.offset_ref
  83.5 0.7 unstack.23.norm_ref
  84.2 0.7 broadcast_in_dim.11.geometry_ref
  84.9 29.7 %panel.2 = (bf16[4,96,2048]{2,1,0:T(8,128)(2,1)}, f32[4,96,2048]{2,1,0:T(8,128)}, bf16[8,16,128,256]{3,2,1,0:T(8,128)(2,1)}) custom-call(s32[1]{0:T(128)} %bitcast.11.side_ref, f32[8192,128]{1,0:T(8,128)} %get-tuple-element.20.pole_ref, f32[8192,128]{1,0:T(8,128)} %get-tuple-element.21.weight_ref, f32[1,2048]{1,0:T(1,128)} %unstack.19.center_ref, ...), custom_call_target="tpu_custom_call" | custom-call | flops 22000001024 | bytes 6291456 | tf_op jit(solution)/shard_map/panel/pallas_call | solution.py:350
  114.6 1.6 collective-permute-start.3
  116.2 29.6 %panel.3 = (bf16[4,96,2048]{2,1,0:T(8,128)(2,1)}, f32[4,96,2048]{2,1,0:T(8,128)}, bf16[8,16,128,256]{3,2,1,0:T(8,128)(2,1)}) custom-call(s32[1]{0:T(128)} %bitcast.11.side_ref, f32[8192,128]{1,0:T(8,128)} %get-tuple-element.20.pole_ref, f32[8192,128]{1,0:T(8,128)} %get-tuple-element.21.weight_ref, f32[1,2048]{1,0:T(1,128)} %unstack.19.center_ref, ...), custom_call_target="tpu_custom_call" | custom-call | flops 22000001024 | bytes 6291456 | tf_op jit(solution)/shard_map/panel/pallas_call | solution.py:350
  145.8 0.4 collective-permute-start.4
  146.2 1.3 dynamic_slice.9
  147.5 0.6 fusion.8
  148.1 0.6 maximum_add_fusion.radius_ref
  148.7 11.3 %update.6.offset_ref.refs_1_ = f32[8,1,128]{2,1,0:T(1,128)} custom-call(s32[2,16]{1,0:T(2,128)} %get-tuple-element.67.near_ref, f32[16]{0:T(128)} %copy-done.4, f32[16]{0:T(128)} %maximum_add_fusion.radius_ref, s32[1]{0:T(128)} %bitcast.6.first_ref, f32[512,128]{1,0:T(8,128)} %bitcast.74, f32[512,128]{1,0:T(8,128)} %bitcast.82, f32[16,1,128]{2,1,0:T(1,128)} %bitcast.99, ...), custom_call_target="tpu_custom_call" | custom-call | flops 10000000000 | bytes 8388608 | tf_op jit(solution)/shard_map/update/pallas_call | solution.py:216
  160.0 1.1 copy-done.6
  161.2 4.3 %merge.2 = (f32[96,2048]{1,0:T(8,128)}, bf16[96,2048]{1,0:T(8,128)(2,1)}, bf16[96,2048]{1,0:T(8,128)(2,1)}, bf16[96,2048]{1,0:T(8,128)(2,1)}) custom-call(s32[1]{0:T(128)} %bitcast.20.deep_ref, f32[4,96,2048]{2,1,0:T(8,128)} %get-tuple-element.25.keep_ref, bf16[4,96,2048]{2,1,0:T(8,128)(2,1)} %copy-done.6), custom_call_target="tpu_custom_call" | custom-call | flops 2000000000 | bytes 6291456 | tf_op jit(solution)/shard_map/merge/pallas_call | solution.py:381
  165.5 1.8 collective-permute-start.5
  167.3 2.4 collective-permute-start.6
  169.7 1.4 collective-permute-start.7
  171.1 13.9 %collective-permute-done.4.met_ref = bf16[4,96,2048]{2,1,0:T(8,128)(2,1)} collective-permute-done((bf16[4,96,2048]{2,1,0:T(8,128)(2,1)}, bf16[4,96,2048]{2,1,0:T(8,128)(2,1)}, u32[]{:S(2)}, u32[]{:S(2)}) %collective-permute-start.4) | collective-permute-done | bytes 1572896 | tf_op jit(solution)/shard_map/ppermute | solution.py:430
  185.0 4.2 %merge.3 = (f32[96,2048]{1,0:T(8,128)}, bf16[96,2048]{1,0:T(8,128)(2,1)}, bf16[96,2048]{1,0:T(8,128)(2,1)}, bf16[96,2048]{1,0:T(8,128)(2,1)}) custom-call(s32[1]{0:T(128)} %bitcast.20.deep_ref, f32[4,96,2048]{2,1,0:T(8,128)} %get-tuple-element.31.keep_ref, bf16[4,96,2048]{2,1,0:T(8,128)(2,1)} %collective-permute-done.4.met_ref), custom_call_target="tpu_custom_call" | custom-call | flops 2000000000 | bytes 6291456 | tf_op jit(solution)/shard_map/merge/pallas_call | solution.py:381
  189.2 3.5 %collective-permute-start.10 = (bf16[96,2048]{1,0:T(8,128)(2,1)}, bf16[96,2048]{1,0:T(8,128)(2,1)S(1)}, u32[]{:S(2)}, u32[]{:S(2)}) collective-permute-start(bf16[96,2048]{1,0:T(8,128)(2,1)} %get-tuple-element.35.refs_4_), channel_id=1, source_target_pairs={{0,24},{4,28},{8,0},{12,4},{16,8},{20,12},{24,16},{28,20},{1,25},{... | collective-permute-start | bytes 1179656 | tf_op jit(solution)/shard_map/ppermute | solution.py:435
  192.7 11.3 %update.7.offset_ref.refs_1_ = f32[8,1,128]{2,1,0:T(1,128)} custom-call(s32[2,16]{1,0:T(2,128)} %get-tuple-element.67.near_ref, f32[16]{0:T(128)} %copy-done.4, f32[16]{0:T(128)} %maximum_add_fusion.radius_ref, s32[1]{0:T(128)} %bitcast.6.first_ref, f32[512,128]{1,0:T(8,128)} %bitcast.75, f32[512,128]{1,0:T(8,128)} %bitcast.83, f32[16,1,128]{2,1,0:T(1,128)} %bitcast.100, ...), custom_call_target="tpu_custom_call" | custom-call | flops 10000000000 | bytes 8388608 | tf_op jit(solution)/shard_map/update/pallas_call | solution.py:216
  204.0 11.3 %update.8.refs_1_ = f32[8,1,128]{2,1,0:T(1,128)} custom-call(s32[2,16]{1,0:T(2,128)} %get-tuple-element.67.near_ref, f32[16]{0:T(128)} %copy-done.4, f32[16]{0:T(128)} %maximum_add_fusion.radius_ref, s32[1]{0:T(128)} %bitcast.6.first_ref, f32[512,128]{1,0:T(8,128)} %bitcast.76, f32[512,128]{1,0:T(8,128)} %bitcast.84, f32[16,1,128]{2,1,0:T(1,128)} %bitcast.101, ...), custom_call_target="tpu_custom_call" | custom-call | flops 10000000000 | bytes 8388608 | tf_op jit(solution)/shard_map/update/pallas_call | solution.py:216
  215.3 11.5 %update.9.offset_ref.refs_1_ = f32[8,1,128]{2,1,0:T(1,128)} custom-call(s32[2,16]{1,0:T(2,128)} %get-tuple-element.67.near_ref, f32[16]{0:T(128)} %copy-done.4, f32[16]{0:T(128)} %maximum_add_fusion.radius_ref, s32[1]{0:T(128)} %bitcast.6.first_ref, f32[512,128]{1,0:T(8,128)} %bitcast.77, f32[512,128]{1,0:T(8,128)} %bitcast.85, f32[16,1,128]{2,1,0:T(1,128)} %bitcast.102, ...), custom_call_target="tpu_custom_call" | custom-call | flops 10000000000 | bytes 8388608 | tf_op jit(solution)/shard_map/update/pallas_call | solution.py:216
  226.8 11.5 %update.10.offset_ref.refs_1_ = f32[8,1,128]{2,1,0:T(1,128)} custom-call(s32[2,16]{1,0:T(2,128)} %get-tuple-element.67.near_ref, f32[16]{0:T(128)} %copy-done.4, f32[16]{0:T(128)} %maximum_add_fusion.radius_ref, s32[1]{0:T(128)} %bitcast.6.first_ref, f32[512,128]{1,0:T(8,128)} %bitcast.78, f32[512,128]{1,0:T(8,128)} %bitcast.86, f32[16,1,128]{2,1,0:T(1,128)} %bitcast.103, ...), custom_call_target="tpu_custom_call" | custom-call | flops 10000000000 | bytes 8388608 | tf_op jit(solution)/shard_map/update/pallas_call | solution.py:216
  238.2 0.0 copy-start.1
  238.2 11.6 %update.11 = f32[8,1,128]{2,1,0:T(1,128)} custom-call(s32[2,16]{1,0:T(2,128)} %get-tuple-element.67.near_ref, f32[16]{0:T(128)} %copy-done.4, f32[16]{0:T(128)} %maximum_add_fusion.radius_ref, s32[1]{0:T(128)} %bitcast.6.first_ref, f32[512,128]{1,0:T(8,128)} %bitcast.79, f32[512,128]{1,0:T(8,128)} %bitcast.87, f32[16,1,128]{2,1,0:T(1,128)} %bitcast.104, ...), custom_call_target="tpu_custom_call" | custom-call | flops 10000000000 | bytes 8388608 | tf_op jit(solution)/shard_map/update/pallas_call | solution.py:216
  249.9 1.3 maximum_bitcast_fusion.refs_0_
  251.1 9.1 %gather.1 = f32[8,16,128]{2,1,0:T(8,128)} custom-call(f32[16,128]{1,0:T(8,128)} %maximum_bitcast_fusion.refs_0_), custom_call_target="tpu_custom_call" | custom-call | tf_op jit(solution)/shard_map/gather/pallas_call | solution.py:76
  260.3 2.3 collective-permute-start.9
  262.5 0.2 add_bitcast_fusion.1
  262.7 15.7 %collective-permute-done.9 = bf16[96,2048]{1,0:T(8,128)(2,1)S(1)} collective-permute-done((bf16[96,2048]{1,0:T(8,128)(2,1)}, bf16[96,2048]{1,0:T(8,128)(2,1)S(1)}, u32[]{:S(2)}, u32[]{:S(2)}) %collective-permute-start.9) | collective-permute-done | bytes 393248 | tf_op jit(solution)/shard_map/ppermute | solution.py:435
  278.4 0.2 add_bitcast_fusion
  278.6 0.1 pad_maximum_fusion
  278.7 2.4 copy.36
  281.1 0.6 copy.40
  (29 shorter events, 0.1 us)
Async XLA Ops:
  2.3 29.3 %all-to-all-start = ((f32[8,2,64,128]{3,2,1,0:T(8,128)}), f32[8,2,64,128]{3,2,1,0:T(8,128)S(1)}, u32[]{:S(2)}, u32[]{:S(2)}) async-start(f32[8,2,64,128]{3,2,1,0:T(8,128)} %broadcast_in_dim.8), calls=%async_computation | async-start | bytes 1048576 | tf_op jit(solution)/shard_map/all_to_all | solution.py:457
  9.5 21.2 %collective-permute-start = (f32[128,128]{1,0:T(8,128)}, f32[128,128]{1,0:T(8,128)S(1)}, u32[]{:S(2)}, u32[]{:S(2)}) collective-permute-start(f32[128,128]{1,0:T(8,128)} %bitcast.93), channel_id=1, source_target_pairs={{0,1},{1,2},{2,3},{3,0},{4,5},{5,6},{6,7},{7,4},{8,9},{9,10},{10,1... | collective-permute-start | bytes 196616 | tf_op jit(solution)/shard_map/ppermute | solution.py:463
  9.5 21.2 %collective-permute-start.1 = (f32[128,128]{1,0:T(8,128)}, f32[128,128]{1,0:T(8,128)S(1)}, u32[]{:S(2)}, u32[]{:S(2)}) collective-permute-start(f32[128,128]{1,0:T(8,128)} %bitcast.94), channel_id=1, source_target_pairs={{0,2},{1,3},{2,0},{3,1},{4,6},{5,7},{6,4},{7,5},{8,10},{9,11},{10,... | collective-permute-start | bytes 196616 | tf_op jit(solution)/shard_map/ppermute | solution.py:463
  11.1 19.6 %collective-permute-start.2 = (f32[128,128]{1,0:T(8,128)}, f32[128,128]{1,0:T(8,128)S(1)}, u32[]{:S(2)}, u32[]{:S(2)}) collective-permute-start(f32[128,128]{1,0:T(8,128)} %bitcast.95), channel_id=1, source_target_pairs={{0,3},{1,0},{2,1},{3,2},{4,7},{5,4},{6,5},{7,6},{8,11},{9,8},{10,9... | collective-permute-start | bytes 196616 | tf_op jit(solution)/shard_map/ppermute | solution.py:463
  13.9 16.8 %copy-start.3 = (f32[16384]{0:T(1024)S(1)}, f32[16384]{0:T(1024)}, u32[]{:S(2)}) copy-start(f32[16384]{0:T(1024)} %param.10) | copy-start | bytes 196612
  30.2 117.9 %copy-start.4 = (f32[16]{0:T(128)}, f32[16]{0:T(128)S(1)}, u32[]{:S(2)}) copy-start(f32[16]{0:T(128)S(1)} %get-tuple-element.57.middle_ref) | copy-start | bytes 196
  58.4 23.6 %all-to-all-start.1 = ((f32[32,8,128]{2,1,0:T(8,128)}), f32[32,8,128]{2,1,0:T(8,128)S(1)}, u32[]{:S(2)}, u32[]{:S(2)}) async-start(f32[32,8,128]{2,1,0:T(8,128)} %broadcast_in_dim.10), calls=%async_computation.1 | async-start | bytes 262144 | tf_op jit(solution)/shard_map/all_to_all | solution.py:457
  114.6 45.5 %collective-permute-start.3 = (bf16[4,96,2048]{2,1,0:T(8,128)(2,1)}, bf16[4,96,2048]{2,1,0:T(8,128)(2,1)S(1)}, u32[]{:S(2)}, u32[]{:S(2)}) collective-permute-start(bf16[4,96,2048]{2,1,0:T(8,128)(2,1)} %get-tuple-element.26), channel_id=1, source_target_pairs={{0,4},{4,0},{8,12},{12,8},{16,20},{20,16},{24,28},{28,24},{1,5},{5... | collective-permute-start | bytes 4718600 | tf_op jit(solution)/shard_map/ppermute | solution.py:430
  145.8 39.2 %collective-permute-start.4 = (bf16[4,96,2048]{2,1,0:T(8,128)(2,1)}, bf16[4,96,2048]{2,1,0:T(8,128)(2,1)}, u32[]{:S(2)}, u32[]{:S(2)}) collective-permute-start(bf16[4,96,2048]{2,1,0:T(8,128)(2,1)} %get-tuple-element.32), channel_id=1, source_target_pairs={{0,4},{4,0},{8,12},{12,8},{16,20},{20,16},{24,28},{28,24},{1,5},{5... | collective-permute-start | bytes 4718600 | tf_op jit(solution)/shard_map/ppermute | solution.py:430
  160.0 1.1 copy-start.6
  165.5 94.7 %collective-permute-start.5 = (bf16[96,2048]{1,0:T(8,128)(2,1)}, bf16[96,2048]{1,0:T(8,128)(2,1)S(1)}, u32[]{:S(2)}, u32[]{:S(2)}) collective-permute-start(bf16[96,2048]{1,0:T(8,128)(2,1)} %get-tuple-element.27.refs_2_), channel_id=1, source_target_pairs={{0,8},{4,12},{8,16},{12,20},{16,24},{20,28},{24,0},{28,4},{1,9},{5... | collective-permute-start | bytes 1179656 | tf_op jit(solution)/shard_map/ppermute | solution.py:435
  167.3 95.2 %collective-permute-start.6 = (bf16[96,2048]{1,0:T(8,128)(2,1)}, bf16[96,2048]{1,0:T(8,128)(2,1)S(1)}, u32[]{:S(2)}, u32[]{:S(2)}) collective-permute-start(bf16[96,2048]{1,0:T(8,128)(2,1)} %get-tuple-element.28.refs_3_), channel_id=1, source_target_pairs={{0,16},{4,20},{8,24},{12,28},{16,0},{20,4},{24,8},{28,12},{1,17},{... | collective-permute-start | bytes 1179656 | tf_op jit(solution)/shard_map/ppermute | solution.py:435
  169.7 92.8 %collective-permute-start.7 = (bf16[96,2048]{1,0:T(8,128)(2,1)}, bf16[96,2048]{1,0:T(8,128)(2,1)S(1)}, u32[]{:S(2)}, u32[]{:S(2)}) collective-permute-start(bf16[96,2048]{1,0:T(8,128)(2,1)} %get-tuple-element.29.refs_4_), channel_id=1, source_target_pairs={{0,24},{4,28},{8,0},{12,4},{16,8},{20,12},{24,16},{28,20},{1,25},{... | collective-permute-start | bytes 1179656 | tf_op jit(solution)/shard_map/ppermute | solution.py:435
  189.2 73.5 %collective-permute-start.10 = (bf16[96,2048]{1,0:T(8,128)(2,1)}, bf16[96,2048]{1,0:T(8,128)(2,1)S(1)}, u32[]{:S(2)}, u32[]{:S(2)}) collective-permute-start(bf16[96,2048]{1,0:T(8,128)(2,1)} %get-tuple-element.35.refs_4_), channel_id=1, source_target_pairs={{0,24},{4,28},{8,0},{12,4},{16,8},{20,12},{24,16},{28,20},{1,25},{... | collective-permute-start | bytes 1179656 | tf_op jit(solution)/shard_map/ppermute | solution.py:435
  192.7 70.0 %collective-permute-start.8 = (bf16[96,2048]{1,0:T(8,128)(2,1)}, bf16[96,2048]{1,0:T(8,128)(2,1)S(1)}, u32[]{:S(2)}, u32[]{:S(2)}) collective-permute-start(bf16[96,2048]{1,0:T(8,128)(2,1)} %get-tuple-element.33.refs_2_), channel_id=1, source_target_pairs={{0,8},{4,12},{8,16},{12,20},{16,24},{20,28},{24,0},{28,4},{1,9},{5... | collective-permute-start | bytes 1179656 | tf_op jit(solution)/shard_map/ppermute | solution.py:435
  238.2 11.6 %copy-start.5 = (f32[8,1,128]{2,1,0:T(1,128)S(1)}, f32[8,1,128]{2,1,0:T(1,128)}, u32[]{:S(2)}) copy-start(f32[8,1,128]{2,1,0:T(1,128)} %update.8.refs_1_) | copy-start | bytes 12292
  238.2 24.3 %copy-start = (f32[96,2048]{1,0:T(8,128)S(1)}, f32[96,2048]{1,0:T(8,128)}, u32[]{:S(2)}) copy-start(f32[96,2048]{1,0:T(8,128)} %get-tuple-element.36) | copy-start | bytes 2359300
  238.2 40.2 %copy-start.1 = (f32[96,2048]{1,0:T(8,128)S(1)}, f32[96,2048]{1,0:T(8,128)}, u32[]{:S(2)}) copy-start(f32[96,2048]{1,0:T(8,128)} %get-tuple-element.37) | copy-start | bytes 2359300
  260.3 18.2 %collective-permute-start.9 = (bf16[96,2048]{1,0:T(8,128)(2,1)}, bf16[96,2048]{1,0:T(8,128)(2,1)S(1)}, u32[]{:S(2)}, u32[]{:S(2)}) collective-permute-start(bf16[96,2048]{1,0:T(8,128)(2,1)} %get-tuple-element.34.refs_3_), channel_id=1, source_target_pairs={{0,16},{4,20},{8,24},{12,28},{16,0},{20,4},{24,8},{28,12},{1,17},{... | collective-permute-start | bytes 1179656 | tf_op jit(solution)/shard_map/ppermute | solution.py:435
  278.4 2.6 copy-start.2

commit v3 on v2

--- a/solution.py
+++ b/solution.py
@@ -12,7 +12,7 @@
 ITERS = 3
 BLOCK = 32
 TERMS = 40
-KAPPA = 8.0
+KAPPA = 4.0
 PAIR = 2
 PIECES = 3
 WIDTH = 256
@@ -91,12 +91,11 @@
         bottom_ref[8 * k : 8 * k + 8, :] = blank
     middle, radius, first, last = geometry
     inverse_radius = 1.0 / radius
-    block = (q * LANES + lax.broadcasted_iota(jnp.int32, (8, LANES), 1)).astype(jnp.float32)
-    far = jnp.logical_or(block < first, block >= last)
-    scale = jnp.where(far, radius, 0.0)
     top, bottom = [], [jnp.ones((8, LANES), jnp.float32)]
     for j in range(BLOCK):
         weight = weights[j : j + 1, :]
+        row = (q * BLOCK + j).astype(jnp.float32)
+        scale = jnp.where(jnp.logical_or(row < first, row >= last), radius, 0.0)
         ratio = scale / (poles[j : j + 1, :] - middle)
         value = (weight * weight) * ratio * inverse_radius
         new_top, new_bottom = [], []
@@ -127,8 +126,7 @@
 
 def update_kernel(count, base, near_ref, middle_ref, radius_ref, first_ref, poles_ref, weights_ref, center_ref, offset_ref, *refs):
     coeff_refs, out_ref = refs[:count], refs[-1]
-    step = pl.program_id(0)
-    tile = base + step
+    tile = base + pl.program_id(0)
     order = lax.broadcasted_iota(jnp.int32, (TERMS, LANES), 0)
     blank = jnp.zeros((8, LANES), jnp.float32)
 
@@ -136,61 +134,64 @@
         high, low = pieces(values)
         return jnp.concatenate([high, high, low, blank], axis=0).T.astype(jnp.bfloat16)
 
-    center, offset = center_ref[0], offset_ref[0]
+    center = center_ref[0]
     middle, radius = middle_ref[tile], radius_ref[tile]
-    place = (center - middle) + offset
-    ratio = jnp.broadcast_to(place / radius, (TERMS, LANES))
-    value_rows = to_rows(power(ratio, order))
-    slope_rows = to_rows(order.astype(jnp.float32) * power(ratio, jnp.maximum(order - 1, 0)))
-    rows = jnp.concatenate([value_rows, slope_rows], axis=0)
-    inverse_sum = square_sum = None
-    for ref, q in [(ref, q) for ref in coeff_refs for q in range(ref.shape[1])]:
-        got = jnp.dot(rows, ref[0, q], preferred_element_type=jnp.float32)
-        top, bottom = got[:LANES, :LANES], got[:LANES, LANES:]
-        top_slope, bottom_slope = got[LANES:, :LANES], got[LANES:, LANES:]
-        inverse = 1.0 / bottom
-        quotient = top * inverse
-        slope = (top_slope - quotient * bottom_slope) * inverse
-        inverse_sum = quotient if inverse_sum is None else inverse_sum + quotient
-        square_sum = slope if square_sum is None else square_sum + slope
-    square_sum = square_sum / radius
-    place_rows = jnp.broadcast_to(place, (LANES, LANES)).T
-    inverse_parts, square_parts = [], []
-    half = LANES // 2
-    for part in range(2):
-        own = slice(part * half, (part + 1) * half)
-        points = place_rows[own]
-
-        def near(step, sums):
-            inverse_sum, square_sum = sums
-            for i in range(PAIR):
-                row = step * PAIR + i
-                pole = poles_ref[pl.ds(row, 1), :] - middle
-                weight = weights_ref[pl.ds(row, 1), :]
-                inverse = 1.0 / (pole - points)
-                weighted = (weight * weight) * inverse
-                inverse_sum = inverse_sum + weighted
-                square_sum = square_sum + weighted * inverse
-            return inverse_sum, square_sum
-
-        sums = lax.fori_loop(near_ref[0, tile], near_ref[1, tile], near, (inverse_sum[own], square_sum[own]))
-        inverse_parts.append(sums[0])
-        square_parts.append(sums[1])
-    total = lambda parts: jnp.sum(jnp.concatenate(parts, axis=0).T, axis=0, keepdims=True)
-    sum_inverse, sum_square = total(inverse_parts), total(square_parts)
-    row = first_ref[0] + tile
-    to_left = poles_ref[pl.ds(row, 1), :] - center
-    final = lax.broadcasted_iota(jnp.int32, (1, LANES), 1) + row * LANES == poles_ref.shape[0] * LANES - 1
-    to_right = jnp.where(final, to_left, -to_left)
-    limit = 0.5 * jnp.minimum(jnp.abs(to_left - offset), jnp.abs(to_right - offset))
-    change = (1.0 + sum_inverse) / sum_square
-    out_ref[0] = offset - jnp.minimum(jnp.maximum(change, -limit), limit)
+
+    def step(_, offset):
+        place = (center - middle) + offset
+        ratio = jnp.broadcast_to(place / radius, (TERMS, LANES))
+        value_rows = to_rows(power(ratio, order))
+        slope_rows = to_rows(order.astype(jnp.float32) * power(ratio, jnp.maximum(order - 1, 0)))
+        rows = jnp.concatenate([value_rows, slope_rows], axis=0)
+        inverse_sum = square_sum = None
+        for ref, q in [(ref, q) for ref in coeff_refs for q in range(ref.shape[1])]:
+            got = jnp.dot(rows, ref[0, q], preferred_element_type=jnp.float32)
+            top, bottom = got[:LANES, :LANES], got[:LANES, LANES:]
+            top_slope, bottom_slope = got[LANES:, :LANES], got[LANES:, LANES:]
+            inverse = 1.0 / bottom
+            quotient = top * inverse
+            slope = (top_slope - quotient * bottom_slope) * inverse
+            inverse_sum = quotient if inverse_sum is None else inverse_sum + quotient
+            square_sum = slope if square_sum is None else square_sum + slope
+        square_sum = square_sum / radius
+        place_rows = jnp.broadcast_to(place, (LANES, LANES)).T
+        inverse_parts, square_parts = [], []
+        half = LANES // 2
+        for part in range(2):
+            own = slice(part * half, (part + 1) * half)
+            points = place_rows[own]
+
+            def near(step, sums):
+                inverse_sum, square_sum = sums
+                for i in range(PAIR):
+                    row = step * PAIR + i
+                    pole = poles_ref[pl.ds(row, 1), :] - middle
+                    weight = weights_ref[pl.ds(row, 1), :]
+                    inverse = 1.0 / (pole - points)
+                    weighted = (weight * weight) * inverse
+                    inverse_sum = inverse_sum + weighted
+                    square_sum = square_sum + weighted * inverse
+                return inverse_sum, square_sum
+
+            sums = lax.fori_loop(near_ref[0, tile], near_ref[1, tile], near, (inverse_sum[own], square_sum[own]))
+            inverse_parts.append(sums[0])
+            square_parts.append(sums[1])
+        total = lambda parts: jnp.sum(jnp.concatenate(parts, axis=0).T, axis=0, keepdims=True)
+        sum_inverse, sum_square = total(inverse_parts), total(square_parts)
+        row = first_ref[0] + tile
+        to_left = poles_ref[pl.ds(row, 1), :] - center
+        final = lax.broadcasted_iota(jnp.int32, (1, LANES), 1) + row * LANES == poles_ref.shape[0] * LANES - 1
+        to_right = jnp.where(final, to_left, -to_left)
+        limit = 0.5 * jnp.minimum(jnp.abs(to_left - offset), jnp.abs(to_right - offset))
+        change = (1.0 + sum_inverse) / sum_square
+        return offset - jnp.minimum(jnp.maximum(change, -limit), limit)
+
+    out_ref[0] = lax.fori_loop(0, ITERS, step, offset_ref[0])
 
 
 def prepare(poles, weights, centers):
     flat = lambda values: values.reshape(-1, LANES)
     tiles = centers.shape[0] // LANES
-    chunks = poles.shape[0] // (BLOCK * LANES)
     tile_centers = flat(centers)
     middle = tile_centers[:, LANES // 2]
     radius = jnp.maximum(tile_centers[:, -1] - middle, middle - tile_centers[:, 0]) + 2.5
@@ -198,34 +199,32 @@
     inside = jnp.sum((poles[None, :] < (middle + KAPPA * radius)[:, None]).astype(jnp.int32), axis=1)
     unit = PAIR * LANES
     near = jnp.stack([below // unit, (inside + unit - 1) // unit])
-    limits = (near * (unit // BLOCK)).astype(jnp.float32)
+    limits = (near * PAIR).astype(jnp.float32)
     geometry = jnp.stack([middle, radius, limits[0], limits[1]])
     geometry = jnp.pad(geometry, ((0, 0), (0, -tiles % 8)), mode="edge")
     geometry = jnp.broadcast_to(geometry[:, :, None], geometry.shape + (LANES,))
-    blocked = lambda values: values.reshape(chunks, LANES, BLOCK).transpose(0, 2, 1)
-    return near, middle, radius, geometry, blocked(poles), blocked(weights)
-
-
-def update(prepared, poles, weights, centers, now, my_first, base, coeffs, after):
-    near, middle, radius = prepared[:3]
-    flat = lambda values: values.reshape(-1, LANES)
+    return near, middle, radius, geometry, flat(poles), flat(weights)
+
+
+def update(prepared, centers, offsets, my_first, base, first, size, coeffs, after):
+    near, middle, radius, _, poles, weights = prepared
     smem, anywhere = pl.BlockSpec(memory_space=pltpu.SMEM), pl.BlockSpec(memory_space=pl.ANY)
-    whole = pl.BlockSpec((poles.shape[0] // LANES, LANES), lambda t: (0, 0))
-    tiles = coeffs[0].shape[0]
-    one = pl.BlockSpec((1, 1, LANES), lambda t: (t, 0, 0))
+    whole = pl.BlockSpec(poles.shape, lambda t: (0, 0))
+    one = pl.BlockSpec((1, 1, LANES), lambda t: (base + t, 0, 0))
+    spread = lambda values: values.reshape(-1, 1, LANES)
     return pl.pallas_call(
         functools.partial(update_kernel, len(coeffs), base),
-        grid=(tiles,),
-        out_shape=jax.ShapeDtypeStruct((tiles, 1, LANES), jnp.float32),
+        grid=(size,),
+        out_shape=jax.ShapeDtypeStruct((size, 1, LANES), jnp.float32),
         in_specs=[smem] * 4
         + [whole] * 2
-        + [pl.BlockSpec((1, 1, LANES), lambda t: (base + t, 0, 0)), one]
-        + [pl.BlockSpec((1,) + c.shape[1:], lambda t: (t, 0, 0, 0)) for c in coeffs]
+        + [one] * 2
+        + [pl.BlockSpec((1,) + c.shape[1:], lambda t: (first + t, 0, 0, 0)) for c in coeffs]
         + [anywhere] * len(after),
-        out_specs=one,
-        cost_estimate=pl.CostEstimate(flops=FLOPS_PER_US * 10, bytes_accessed=tiles * LANES * LANES * 64, transcendentals=0),
+        out_specs=pl.BlockSpec((1, 1, LANES), lambda t: (t, 0, 0)),
+        cost_estimate=pl.CostEstimate(flops=FLOPS_PER_US * 15, bytes_accessed=size * LANES * LANES * 64, transcendentals=0),
         name="update",
-    )(near, middle, radius, (my_first // LANES).reshape(1), flat(poles), flat(weights), centers.reshape(-1, 1, LANES), now, *coeffs, *after)
+    )(near, middle, radius, (my_first // LANES).reshape(1), poles, weights, spread(centers), spread(offsets), *coeffs, *after)
 
 
 def lookup_kernel(index_ref, *refs):
@@ -272,10 +271,9 @@
     )(index.reshape(groups, 1, LANES), *tables)
 
 
-def chosen_kernel(poles_ref, weights_ref, last_ref, left_ref, right_ref, start_ref, out_ref):
-    count = last_ref.shape[0]
-    left, right = left_ref[:count], right_ref[:count]
-    center = jnp.where(last_ref[...] > 0, left + 0.5, 0.5 * (left + right))
+def chosen_kernel(count, poles_ref, weights_ref, found_ref, start_ref, out_ref):
+    left, right = found_ref[:count], found_ref[LANES : LANES + count]
+    center = jnp.where(left == right, left + 0.5, 0.5 * (left + right))
     to_left, to_right = left - center, right - center
     rows = poles_ref.shape[0]
 
@@ -297,7 +295,7 @@
         change = (1.0 + sum_inverse) / sum_square
         return offset - jnp.minimum(jnp.maximum(change, -limit), limit)
 
-    offset = lax.fori_loop(0, ITERS, step, start_ref[:count])
+    offset = lax.fori_loop(0, ITERS, step, start_ref[2 * LANES : 2 * LANES + count])
     norm = lax.rsqrt(sweep(offset, True)[1])
     lane = lax.broadcasted_iota(jnp.int32, (count, LANES), 1)
     own = lane == lax.broadcasted_iota(jnp.int32, (count, LANES), 0)
@@ -323,7 +321,8 @@
     for u in range(per):
         q = lax.rem(start + pl.program_id(0) * per + u, chunks)
         geometry = [geometry_ref[i] for i in range(4)]
-        coefficients(geometry, block_poles_ref[u], block_weights_ref[u], q, coeff_ref, u, *refs[2 * u : 2 * u + 2])
+        own = pl.ds(u * BLOCK, BLOCK)
+        coefficients(geometry, block_poles_ref[own, :], block_weights_ref[own, :], q, coeff_ref, u, *refs[2 * u : 2 * u + 2])
     total_ref[...] = total
     side = side_ref[0]
     size = send_ref.shape[1]
@@ -337,7 +336,7 @@
     width = panel[0].shape[0]
     steps = width // WIDTH
     geometry, block_poles, block_weights = prepared[3:]
-    chunks = block_poles.shape[0]
+    chunks = block_poles.shape[0] // BLOCK
     octets = geometry.shape[1] // 8
     per = octets * chunks // (eigen.shape[0] * steps)
     start = half * steps * per
@@ -346,7 +345,7 @@
     row = pl.BlockSpec((1, WIDTH), lambda i: (0, i))
     wide = pl.BlockSpec((depth, LANES), lambda i: (half, 0))
     out = pl.BlockSpec(shape[:2] + (WIDTH,), lambda i: (0, 0, i))
-    blocks = pl.BlockSpec((per, BLOCK, LANES), lambda i: (start % chunks // per + i, 0, 0))
+    blocks = pl.BlockSpec((per * BLOCK, LANES), lambda i: (start % chunks // per + i, 0))
     return pl.pallas_call(
         functools.partial(panel_kernel, start, chunks),
         grid=(steps,),
@@ -406,11 +405,10 @@
     turned = lax.rem(col - padded // per_col + cols, cols) * per_col + lax.rem(padded, per_col)
     index = jnp.concatenate([padded, jnp.minimum(padded + 1, total - 1), turned])
     found_pole, found_offset = lookup([flat(all_poles), all_offsets], index)
-    last = jnp.broadcast_to((mine == total - 1).astype(jnp.int32)[:, None], (share, LANES))
     here = pl.BlockSpec(memory_space=pltpu.VMEM)
     packed = pl.pallas_call(
-        chosen_kernel, out_shape=jax.ShapeDtypeStruct((8, LANES), jnp.float32), in_specs=[here] * 6, out_specs=here, name="chosen"
-    )(flat(all_poles), flat(all_weights), last, found_pole[:LANES], found_pole[LANES : 2 * LANES], found_offset[2 * LANES :])
+        functools.partial(chosen_kernel, share), out_shape=jax.ShapeDtypeStruct((8, LANES), jnp.float32), in_specs=[here] * 4, out_specs=here, name="chosen"
+    )(flat(all_poles), flat(all_weights), found_pole, found_offset)
     shared = copies(packed, AXES, rows * cols)
     panel = shared[:, :3, :share].transpose(1, 0, 2).reshape(3, -1)
 
@@ -438,15 +436,15 @@
 
     members = coeffs[0].shape[0]
     groups = [coeffs] if members == tiles else [[c] for c in coeffs]
-    calls = [(g, step) for g in range(len(groups)) for step in range(ITERS)]
-    lates = {1: outgoing[0], len(calls) // 2: outgoing[1]}
-    latest = []
-    spread = my_offsets.reshape(tiles, 1, LANES)
-    nows = [spread[g * members : (g + 1) * members] for g in range(len(groups))]
-    for at, (g, step) in enumerate(calls):
-        nows[g] = update(prepared, all_poles, all_weights, my_centers, nows[g], my_first, g * members, groups[g], latest + lates.get(at, []))
-        latest = [nows[g]]
-    my_offsets = jnp.concatenate(nows, axis=0)
+    size = max(members // 2, 1)
+    calls = [(g, first) for g in range(len(groups)) for first in range(0, members, size)]
+    lates = {1: outgoing[0], 2: outgoing[1]}
+    found, latest = [], []
+    for at, (g, first) in enumerate(calls):
+        after = latest + lates.get(at, [])
+        latest = [update(prepared, my_centers, my_offsets, my_first, g * members + first, first, size, groups[g], after)]
+        found += latest
+    my_offsets = jnp.concatenate(found, axis=0)
     offset_now = gather([(flat(my_offsets), ("row",))], 2)[0].reshape(-1)
     add = lambda parts: sum([p.astype(jnp.float32) for p in parts[1:]], parts[0])
     halves = [add(parts) for parts in received]

time: 284 us -> 265 us (0.933)
  Pallas kernels: 178 us -> 168 us
  local copies, waits for them, and re-layouts: 36.7 us -> 29.3 us
    pallas_call x6 -> x4, Pallas kernels: 68.5 us -> 58 us  [update(): pl.pallas_call(functools.partial(update_kernel, len(coeffs), base), grid=...]
    another operation x4 -> x0, local copies, waits for them, and re-layouts: 4.46 us -> none  [prepare(): values.reshape(chunks, LANES, BLOCK).transpose(0, 2, 1)]
    slice x3 -> x0, local copies, waits for them, and re-layouts: 3.59 us -> none  [the longest x1 1.52 us: on_device(): found_pole[LANES:2 * LANES]]
    unnamed x17 -> x21, local copies, waits for them, and re-layouts: 18.7 us -> 18.7 us
  transfers between devices with their start and end apart: 13 -> 13, of which waited for: 2 -> 2; matrix products, arithmetic and copies ran while one was open for 11% -> 10% of each run, Pallas kernels for 45% -> 44%
where the time goes in v3:
time: 265 us; the launch traced here: 264 us
  Pallas kernels  168 us (63%)
  waiting for transfers between devices  29.9 us (11%)
  local copies, waits for them, and re-layouts  29.3 us (11%)
  starting transfers between devices  29.1 us (11%)
  other arithmetic  7.17 us (3%)
    pallas_call x2, Pallas kernels, panel_half(): pl.pallas_call(functools.partial(panel_kernel, start, chunks), grid=(step...  59.8 us
    pallas_call x4, Pallas kernels, update(): pl.pallas_call(functools.partial(update_kernel, len(coeffs), base), grid=...  58 us
    unnamed x21, local copies, waits for them, and re-layouts  18.7 us
    pallas_call x1, Pallas kernels, on_device(): pl.pallas_call(functools.partial(chosen_kernel, share), out_shape=jax.Sha...  18.6 us
    ppermute x6, waiting for transfers between devices, on_device(): arrived.append(lax.ppermute(block, 'row', pairs))  15.7 us
    ppermute x2, waiting for transfers between devices, on_device(): met = lax.ppermute(send, 'row', near_pairs)  14.2 us
    pallas_call x2, Pallas kernels, lookup(): pl.pallas_call(lookup_kernel, grid=(groups // step,), out_shape=[jax.Shap...  13.8 us
    ppermute x6, starting transfers between devices, on_device(): arrived.append(lax.ppermute(block, 'row', pairs))  11.4 us
  transfers between devices with their start and end apart: 13, of which 2 were waited for; matrix products, arithmetic and copies ran while one was open for 10% of the time, Pallas kernels for 44%

profile of v3, /device:TPU:0, one launch (start us, length us, event | category | flops | bytes accessed | tf_op | source)
XLA Modules:
  0.0 263.9 jit_solution(6340936485879803005)
XLA Ops:
  0.6 0.5 collective-permute-start
  1.2 2.6 collective-permute-start.1
  3.8 1.4 collective-permute-start.2
  5.1 0.8 pad_maximum_fusion.2
  5.9 0.8 broadcast_in_dim.6
  6.8 5.8 %all-to-all-start = ((f32[8,2,64,128]{3,2,1,0:T(8,128)}), f32[8,2,64,128]{3,2,1,0:T(8,128)S(1)}, u32[]{:S(2)}, u32[]{:S(2)}) async-start(f32[8,2,64,128]{3,2,1,0:T(8,128)} %broadcast_in_dim.6), calls=%async_computation | async-start | bytes 1048576 | tf_op jit(solution)/shard_map/all_to_all | solution.py:455
  12.6 0.8 dynamic_slice.11
  13.4 1.4 reshape_reshape.3.index_ref
  14.8 14.5 %copy.40 = bf16[768,2,4096]{2,0,1:T(8,128)(2,1)} copy(bf16[768,2,4096]{2,1,0:T(2,128)(2,1)} %param.13) | data formatting | bytes 25165824 | tf_op args[6]
  29.3 0.6 dynamic_slice.10
  29.9 1.3 dynamic_slice.9
  31.2 0.7 dynamic-slice_bitcast_fusion
  31.9 0.2 slice_reduce_fusion.4
  32.1 0.5 maximum_add_fusion.radius_ref
  32.7 0.6 pad_add_fusion.index_ref
  33.3 0.0 collective-permute-done
  33.3 0.0 collective-permute-done.1
  33.3 0.0 collective-permute-done.2
  33.3 0.7 pad_maximum_fusion.1.refs_1_
  34.0 0.0 all-to-all-done
  34.0 0.9 fusion.6
  34.9 2.5 lookup.3
  37.4 18.6 %chosen.1 = f32[8,128]{1,0:T(8,128)} custom-call(f32[512,128]{1,0:T(8,128)} %bitcast.66, f32[512,128]{1,0:T(8,128)} %bitcast.75, f32[384,128]{1,0:T(8,128)} %get-tuple-element.22.found_ref, f32[384,128]{1,0:T(8,128)} %get-tuple-element.23.start_ref), custom_call_target="tpu_custom_call" | custom-call | tf_op jit(solution)/shard_map/chosen/pallas_call | solution.py:409
  56.0 1.3 broadcast_in_dim.7
  57.4 5.3 %all-to-all-start.1 = ((f32[32,8,128]{2,1,0:T(8,128)}), f32[32,8,128]{2,1,0:T(8,128)S(1)}, u32[]{:S(2)}, u32[]{:S(2)}) async-start(f32[32,8,128]{2,1,0:T(8,128)} %broadcast_in_dim.7), calls=%async_computation.1 | async-start | bytes 262144 | tf_op jit(solution)/shard_map/all_to_all | solution.py:455
  62.6 1.9 convert_reduce_fusion.1
  64.6 11.3 %lookup.2 = (f32[8192,128]{1,0:T(8,128)}, f32[8192,128]{1,0:T(8,128)}) custom-call(s32[64,1,128]{2,1,0:T(1,128)} %reshape_reshape.3.index_ref, f32[512,128]{1,0:T(8,128)} %bitcast.68, f32[512,128]{1,0:T(8,128)} %bitcast.76), custom_call_target="tpu_custom_call" | custom-call | tf_op jit(solution)/shard_map/lookup/pallas_call | solution.py:263
  75.9 0.6 multiply_convert_fusion
  76.5 0.0 all-to-all-done.1
  76.5 0.1 slice_reduce_fusion
  76.7 0.7 unstack.19.center_ref
  77.3 0.7 unstack.21.offset_ref
  78.0 0.7 unstack.23.norm_ref
  78.7 0.7 broadcast_in_dim.8.geometry_ref
  79.4 29.9 %panel.2 = (bf16[4,96,2048]{2,1,0:T(8,128)(2,1)}, f32[4,96,2048]{2,1,0:T(8,128)}, bf16[8,16,128,256]{3,2,1,0:T(8,128)(2,1)}) custom-call(s32[1]{0:T(128)} %bitcast.11.side_ref, f32[8192,128]{1,0:T(8,128)} %get-tuple-element.20.pole_ref, f32[8192,128]{1,0:T(8,128)} %get-tuple-element.21.weight_ref, f32[1,2048]{1,0:T(1,128)} %unstack.19.center_ref, ...), custom_call_target="tpu_custom_call" | custom-call | flops 22000001024 | bytes 6291456 | tf_op jit(solution)/shard_map/panel/pallas_call | solution.py:349
  109.3 1.7 collective-permute-start.3
  110.9 29.9 %panel.3 = (bf16[4,96,2048]{2,1,0:T(8,128)(2,1)}, f32[4,96,2048]{2,1,0:T(8,128)}, bf16[8,16,128,256]{3,2,1,0:T(8,128)(2,1)}) custom-call(s32[1]{0:T(128)} %bitcast.11.side_ref, f32[8192,128]{1,0:T(8,128)} %get-tuple-element.20.pole_ref, f32[8192,128]{1,0:T(8,128)} %get-tuple-element.21.weight_ref, f32[1,2048]{1,0:T(1,128)} %unstack.19.center_ref, ...), custom_call_target="tpu_custom_call" | custom-call | flops 22000001024 | bytes 6291456 | tf_op jit(solution)/shard_map/panel/pallas_call | solution.py:349
  140.8 0.4 collective-permute-start.4
  141.3 14.2 %update.4.refs_1_ = f32[4,1,128]{2,1,0:T(1,128)} custom-call(s32[2,16]{1,0:T(2,128)} %get-tuple-element.61.near_ref, f32[16]{0:T(128)} %copy-done.4, f32[16]{0:T(128)} %maximum_add_fusion.radius_ref, s32[1]{0:T(128)} %bitcast.6.first_ref, f32[512,128]{1,0:T(8,128)} %bitcast.71, f32[512,128]{1,0:T(8,128)} %bitcast.79, f32[16,1,128]{2,1,0:T(1,128)} %bitcast.94, ...), custom_call_target="tpu_custom_call" | custom-call | flops 15000000512 | bytes 4194304 | tf_op jit(solution)/shard_map/update/pallas_call | solution.py:215
  155.5 0.0 collective-permute-done.3.met_ref
  155.5 4.3 %merge.2 = (f32[96,2048]{1,0:T(8,128)}, bf16[96,2048]{1,0:T(8,128)(2,1)}, bf16[96,2048]{1,0:T(8,128)(2,1)}, bf16[96,2048]{1,0:T(8,128)(2,1)}) custom-call(s32[1]{0:T(128)} %bitcast.19.deep_ref, f32[4,96,2048]{2,1,0:T(8,128)} %get-tuple-element.25.keep_ref, bf16[4,96,2048]{2,1,0:T(8,128)(2,1)} %collective-permute-done.3.met_ref), custom_call_target="tpu_custom_call" | custom-call | flops 2000000000 | bytes 6291456 | tf_op jit(solution)/shard_map/merge/pallas_call | solution.py:380
  159.8 1.9 collective-permute-start.5
  161.7 2.4 collective-permute-start.6
  164.1 1.4 collective-permute-start.7
  165.5 14.1 %collective-permute-done.4.met_ref = bf16[4,96,2048]{2,1,0:T(8,128)(2,1)S(1)} collective-permute-done((bf16[4,96,2048]{2,1,0:T(8,128)(2,1)}, bf16[4,96,2048]{2,1,0:T(8,128)(2,1)S(1)}, u32[]{:S(2)}, u32[]{:S(2)}) %collective-permute-start.4) | collective-permute-done | bytes 1572896 | tf_op jit(solution)/shard_map/ppermute | solution.py:428
  179.6 1.1 copy-done.8
  180.8 4.3 %merge.3 = (f32[96,2048]{1,0:T(8,128)}, bf16[96,2048]{1,0:T(8,128)(2,1)}, bf16[96,2048]{1,0:T(8,128)(2,1)}, bf16[96,2048]{1,0:T(8,128)(2,1)}) custom-call(s32[1]{0:T(128)} %bitcast.19.deep_ref, f32[4,96,2048]{2,1,0:T(8,128)} %get-tuple-element.31.keep_ref, bf16[4,96,2048]{2,1,0:T(8,128)(2,1)} %copy-done.8), custom_call_target="tpu_custom_call" | custom-call | flops 2000000000 | bytes 6291456 | tf_op jit(solution)/shard_map/merge/pallas_call | solution.py:380
  185.1 3.5 %collective-permute-start.10 = (bf16[96,2048]{1,0:T(8,128)(2,1)}, bf16[96,2048]{1,0:T(8,128)(2,1)S(1)}, u32[]{:S(2)}, u32[]{:S(2)}) collective-permute-start(bf16[96,2048]{1,0:T(8,128)(2,1)} %get-tuple-element.35.refs_4_), channel_id=1, source_target_pairs={{0,24},{4,28},{8,0},{12,4},{16,8},{20,12},{24,16},{28,20},{1,25},{... | collective-permute-start | bytes 1179656 | tf_op jit(solution)/shard_map/ppermute | solution.py:433
  188.6 0.0 collective-permute-start.8
  188.6 14.5 %update.5.refs_1_ = f32[4,1,128]{2,1,0:T(1,128)} custom-call(s32[2,16]{1,0:T(2,128)} %get-tuple-element.61.near_ref, f32[16]{0:T(128)} %copy-done.4, f32[16]{0:T(128)} %maximum_add_fusion.radius_ref, s32[1]{0:T(128)} %bitcast.6.first_ref, f32[512,128]{1,0:T(8,128)} %bitcast.72, f32[512,128]{1,0:T(8,128)} %bitcast.80, f32[16,1,128]{2,1,0:T(1,128)} %bitcast.95, ...), custom_call_target="tpu_custom_call" | custom-call | flops 15000000512 | bytes 4194304 | tf_op jit(solution)/shard_map/update/pallas_call | solution.py:215
  203.1 14.6 %update.6.refs_1_ = f32[4,1,128]{2,1,0:T(1,128)} custom-call(s32[2,16]{1,0:T(2,128)} %get-tuple-element.61.near_ref, f32[16]{0:T(128)} %copy-done.4, f32[16]{0:T(128)} %maximum_add_fusion.radius_ref, s32[1]{0:T(128)} %bitcast.6.first_ref, f32[512,128]{1,0:T(8,128)} %bitcast.73, f32[512,128]{1,0:T(8,128)} %bitcast.81, f32[16,1,128]{2,1,0:T(1,128)} %bitcast.96, ...), custom_call_target="tpu_custom_call" | custom-call | flops 15000000512 | bytes 4194304 | tf_op jit(solution)/shard_map/update/pallas_call | solution.py:215
  217.7 14.7 %update.7 = f32[4,1,128]{2,1,0:T(1,128)} custom-call(s32[2,16]{1,0:T(2,128)} %get-tuple-element.61.near_ref, f32[16]{0:T(128)} %copy-done.4, f32[16]{0:T(128)} %maximum_add_fusion.radius_ref, s32[1]{0:T(128)} %bitcast.6.first_ref, f32[512,128]{1,0:T(8,128)} %bitcast.74, f32[512,128]{1,0:T(8,128)} %bitcast.82, f32[16,1,128]{2,1,0:T(1,128)} %bitcast.97, ...), custom_call_target="tpu_custom_call" | custom-call | flops 15000000512 | bytes 4194304 | tf_op jit(solution)/shard_map/update/pallas_call | solution.py:215
  232.4 1.3 maximum_bitcast_fusion.refs_0_
  233.7 8.7 %gather.1 = f32[8,16,128]{2,1,0:T(8,128)} custom-call(f32[16,128]{1,0:T(8,128)} %maximum_bitcast_fusion.refs_0_), custom_call_target="tpu_custom_call" | custom-call | tf_op jit(solution)/shard_map/gather/pallas_call | solution.py:76
  242.4 0.0 collective-permute-done.5
  242.5 2.3 collective-permute-start.9
  244.7 0.0 collective-permute-done.6
  244.7 0.2 add_bitcast_fusion.1
  244.9 0.0 collective-permute-done.10
  244.9 15.7 %collective-permute-done.9 = bf16[96,2048]{1,0:T(8,128)(2,1)S(1)} collective-permute-done((bf16[96,2048]{1,0:T(8,128)(2,1)}, bf16[96,2048]{1,0:T(8,128)(2,1)S(1)}, u32[]{:S(2)}, u32[]{:S(2)}) %collective-permute-start.9) | collective-permute-done | bytes 393248 | tf_op jit(solution)/shard_map/ppermute | solution.py:433
  260.6 0.2 add_bitcast_fusion
  260.8 0.1 pad_maximum_fusion
  260.9 2.4 copy.38
  263.3 0.6 copy.42
  (24 shorter events, 0.1 us)
Async XLA Ops:
  0.6 32.6 %collective-permute-start = (f32[128,128]{1,0:T(8,128)}, f32[128,128]{1,0:T(8,128)S(1)}, u32[]{:S(2)}, u32[]{:S(2)}) collective-permute-start(f32[128,128]{1,0:T(8,128)} %bitcast.84), channel_id=1, source_target_pairs={{0,1},{1,2},{2,3},{3,0},{4,5},{5,6},{6,7},{7,4},{8,9},{9,10},{10,1... | collective-permute-start | bytes 196616 | tf_op jit(solution)/shard_map/ppermute | solution.py:461
  1.2 32.1 %collective-permute-start.1 = (f32[128,128]{1,0:T(8,128)}, f32[128,128]{1,0:T(8,128)S(1)}, u32[]{:S(2)}, u32[]{:S(2)}) collective-permute-start(f32[128,128]{1,0:T(8,128)} %bitcast.85), channel_id=1, source_target_pairs={{0,2},{1,3},{2,0},{3,1},{4,6},{5,7},{6,4},{7,5},{8,10},{9,11},{10,... | collective-permute-start | bytes 196616 | tf_op jit(solution)/shard_map/ppermute | solution.py:461
  3.8 29.5 %collective-permute-start.2 = (f32[128,128]{1,0:T(8,128)}, f32[128,128]{1,0:T(8,128)S(1)}, u32[]{:S(2)}, u32[]{:S(2)}) collective-permute-start(f32[128,128]{1,0:T(8,128)} %bitcast.86), channel_id=1, source_target_pairs={{0,3},{1,0},{2,1},{3,2},{4,7},{5,4},{6,5},{7,6},{8,11},{9,8},{10,9... | collective-permute-start | bytes 196616 | tf_op jit(solution)/shard_map/ppermute | solution.py:461
  6.8 27.2 %all-to-all-start = ((f32[8,2,64,128]{3,2,1,0:T(8,128)}), f32[8,2,64,128]{3,2,1,0:T(8,128)S(1)}, u32[]{:S(2)}, u32[]{:S(2)}) async-start(f32[8,2,64,128]{3,2,1,0:T(8,128)} %broadcast_in_dim.6), calls=%async_computation | async-start | bytes 1048576 | tf_op jit(solution)/shard_map/all_to_all | solution.py:455
  14.8 14.5 %copy-start.3 = (f32[16384]{0:T(1024)S(1)}, f32[16384]{0:T(1024)}, u32[]{:S(2)}) copy-start(f32[16384]{0:T(1024)} %param.10) | copy-start | bytes 196612
  32.1 77.2 %copy-start.4 = (f32[16]{0:T(128)}, f32[16]{0:T(128)S(1)}, u32[]{:S(2)}) copy-start(f32[16]{0:T(128)S(1)} %get-tuple-element.57.middle_ref) | copy-start | bytes 196
  57.4 19.1 %all-to-all-start.1 = ((f32[32,8,128]{2,1,0:T(8,128)}), f32[32,8,128]{2,1,0:T(8,128)S(1)}, u32[]{:S(2)}, u32[]{:S(2)}) async-start(f32[32,8,128]{2,1,0:T(8,128)} %broadcast_in_dim.7), calls=%async_computation.1 | async-start | bytes 262144 | tf_op jit(solution)/shard_map/all_to_all | solution.py:455
  109.3 46.2 %collective-permute-start.3 = (bf16[4,96,2048]{2,1,0:T(8,128)(2,1)}, bf16[4,96,2048]{2,1,0:T(8,128)(2,1)}, u32[]{:S(2)}, u32[]{:S(2)}) collective-permute-start(bf16[4,96,2048]{2,1,0:T(8,128)(2,1)} %get-tuple-element.26), channel_id=1, source_target_pairs={{0,4},{4,0},{8,12},{12,8},{16,20},{20,16},{24,28},{28,24},{1,5},{5... | collective-permute-start | bytes 4718600 | tf_op jit(solution)/shard_map/ppermute | solution.py:428
  140.8 38.8 %collective-permute-start.4 = (bf16[4,96,2048]{2,1,0:T(8,128)(2,1)}, bf16[4,96,2048]{2,1,0:T(8,128)(2,1)S(1)}, u32[]{:S(2)}, u32[]{:S(2)}) collective-permute-start(bf16[4,96,2048]{2,1,0:T(8,128)(2,1)} %get-tuple-element.32), channel_id=1, source_target_pairs={{0,4},{4,0},{8,12},{12,8},{16,20},{20,16},{24,28},{28,24},{1,5},{5... | collective-permute-start | bytes 4718600 | tf_op jit(solution)/shard_map/ppermute | solution.py:428
  159.8 82.7 %collective-permute-start.5 = (bf16[96,2048]{1,0:T(8,128)(2,1)}, bf16[96,2048]{1,0:T(8,128)(2,1)S(1)}, u32[]{:S(2)}, u32[]{:S(2)}) collective-permute-start(bf16[96,2048]{1,0:T(8,128)(2,1)} %get-tuple-element.27.refs_2_), channel_id=1, source_target_pairs={{0,8},{4,12},{8,16},{12,20},{16,24},{20,28},{24,0},{28,4},{1,9},{5... | collective-permute-start | bytes 1179656 | tf_op jit(solution)/shard_map/ppermute | solution.py:433
  161.7 83.0 %collective-permute-start.6 = (bf16[96,2048]{1,0:T(8,128)(2,1)}, bf16[96,2048]{1,0:T(8,128)(2,1)S(1)}, u32[]{:S(2)}, u32[]{:S(2)}) collective-permute-start(bf16[96,2048]{1,0:T(8,128)(2,1)} %get-tuple-element.28.refs_3_), channel_id=1, source_target_pairs={{0,16},{4,20},{8,24},{12,28},{16,0},{20,4},{24,8},{28,12},{1,17},{... | collective-permute-start | bytes 1179656 | tf_op jit(solution)/shard_map/ppermute | solution.py:433
  164.1 80.6 %collective-permute-start.7 = (bf16[96,2048]{1,0:T(8,128)(2,1)}, bf16[96,2048]{1,0:T(8,128)(2,1)S(1)}, u32[]{:S(2)}, u32[]{:S(2)}) collective-permute-start(bf16[96,2048]{1,0:T(8,128)(2,1)} %get-tuple-element.29.refs_4_), channel_id=1, source_target_pairs={{0,24},{4,28},{8,0},{12,4},{16,8},{20,12},{24,16},{28,20},{1,25},{... | collective-permute-start | bytes 1179656 | tf_op jit(solution)/shard_map/ppermute | solution.py:433
  179.6 1.1 copy-start.8
  185.1 59.8 %collective-permute-start.10 = (bf16[96,2048]{1,0:T(8,128)(2,1)}, bf16[96,2048]{1,0:T(8,128)(2,1)S(1)}, u32[]{:S(2)}, u32[]{:S(2)}) collective-permute-start(bf16[96,2048]{1,0:T(8,128)(2,1)} %get-tuple-element.35.refs_4_), channel_id=1, source_target_pairs={{0,24},{4,28},{8,0},{12,4},{16,8},{20,12},{24,16},{28,20},{1,25},{... | collective-permute-start | bytes 1179656 | tf_op jit(solution)/shard_map/ppermute | solution.py:433
  188.6 56.3 %collective-permute-start.8 = (bf16[96,2048]{1,0:T(8,128)(2,1)}, bf16[96,2048]{1,0:T(8,128)(2,1)S(1)}, u32[]{:S(2)}, u32[]{:S(2)}) collective-permute-start(bf16[96,2048]{1,0:T(8,128)(2,1)} %get-tuple-element.33.refs_2_), channel_id=1, source_target_pairs={{0,8},{4,12},{8,16},{12,20},{16,24},{20,28},{24,0},{28,4},{1,9},{5... | collective-permute-start | bytes 1179656 | tf_op jit(solution)/shard_map/ppermute | solution.py:433
  217.6 14.8 %copy-start.5 = (f32[4,1,128]{2,1,0:T(1,128)S(1)}, f32[4,1,128]{2,1,0:T(1,128)}, u32[]{:S(2)}) copy-start(f32[4,1,128]{2,1,0:T(1,128)} %update.4.refs_1_) | copy-start | bytes 6148
  217.6 14.8 %copy-start.6 = (f32[4,1,128]{2,1,0:T(1,128)S(1)}, f32[4,1,128]{2,1,0:T(1,128)}, u32[]{:S(2)}) copy-start(f32[4,1,128]{2,1,0:T(1,128)} %update.5.refs_1_) | copy-start | bytes 6148
  217.6 14.8 %copy-start.7 = (f32[4,1,128]{2,1,0:T(1,128)S(1)}, f32[4,1,128]{2,1,0:T(1,128)}, u32[]{:S(2)}) copy-start(f32[4,1,128]{2,1,0:T(1,128)} %update.6.refs_1_) | copy-start | bytes 6148
  217.7 27.1 %copy-start = (f32[96,2048]{1,0:T(8,128)S(1)}, f32[96,2048]{1,0:T(8,128)}, u32[]{:S(2)}) copy-start(f32[96,2048]{1,0:T(8,128)} %get-tuple-element.36) | copy-start | bytes 2359300
  217.7 43.0 %copy-start.1 = (f32[96,2048]{1,0:T(8,128)S(1)}, f32[96,2048]{1,0:T(8,128)}, u32[]{:S(2)}) copy-start(f32[96,2048]{1,0:T(8,128)} %get-tuple-element.37) | copy-start | bytes 2359300
  242.5 18.2 %collective-permute-start.9 = (bf16[96,2048]{1,0:T(8,128)(2,1)}, bf16[96,2048]{1,0:T(8,128)(2,1)S(1)}, u32[]{:S(2)}, u32[]{:S(2)}) collective-permute-start(bf16[96,2048]{1,0:T(8,128)(2,1)} %get-tuple-element.34.refs_3_), channel_id=1, source_target_pairs={{0,16},{4,20},{8,24},{12,28},{16,0},{20,4},{24,8},{28,12},{1,17},{... | collective-permute-start | bytes 1179656 | tf_op jit(solution)/shard_map/ppermute | solution.py:433
  260.6 2.6 %copy-start.2 = (f32[8,16,128]{2,1,0:T(8,128)S(1)}, f32[8,16,128]{2,1,0:T(8,128)}, u32[]{:S(2)}) copy-start(f32[8,16,128]{2,1,0:T(8,128)} %gather.1) | copy-start | bytes 196612
